TPU v7x, 256 devices: a whole 4x4x8 slice. The times are simulated.
256 devices in a mesh: obs: 64 (over z, x, core), bel: 4 (over y).
Axes of the slice: x: 4, y: 4, z: 8, core: 2. Of those that a mesh axis runs over, the one named last changes fastest.
Arguments:
- alpha_set: bfloat16 [2048, 2048], P('bel'), may hold values from -600 to 600
- transitions: bfloat16 [16, 2048, 2048], P(None, 'obs'), may hold values from 0.0009994507 to 1
- obs_weights: float32 [256, 16, 2048], P('obs'), may hold values from 0.01 to 1
- rewards: float32 [16, 2048], replicated, may hold values from -1 to 1
- chosen_idx: int32 [1536, 16, 256], P('bel', None, 'obs'), may hold values from 0 to 2047
- chosen_action: int32 [1536], P('bel'), may hold values from 0 to 15
Outputs:
- new_alpha: float32 [1536, 2048], P(('bel', 'obs'))
Inputs may be any that keep to these rules, and one draw needn't show every extreme that they name: `chosen_idx`: an index into the 2048 alpha vectors. `chosen_action`: an index into the 16 actions.
All inputs are finite; a program needn't handle non-finite values.
Results may differ from a plain program's by a relative error of at most 0.0003.
Values may be sent and summed in bfloat16 or wider, within the bound.
A program may use at most 64 MiB of HBM per device.

v0:
```python
import jax
import jax.numpy as jnp
from jax import lax
from jax.sharding import Mesh
from jax.sharding import PartitionSpec as P

OBS = ("obs_0", "obs_1", "obs_2")
BEL_OBS = ("bel", "obs_0", "obs_1", "obs_2")


discount = 0.95


def over_pieces(x, axis):
    blocks = lax.all_gather(x, axis)
    return blocks.sum(axis=0)


def in_blocks(x, dim, peers):
    dims = x.shape
    blocks = x.reshape(*dims[:dim], peers, dims[dim] // peers, *dims[dim + 1 :])
    return jnp.moveaxis(blocks, dim, 0)


def sent_and_summed(x, axis, dim):
    blocks = in_blocks(x, dim, lax.axis_size(axis))
    arrived = lax.all_to_all(blocks, axis, split_axis=0, concat_axis=0, tiled=True)
    return arrived.sum(axis=0)


def in_one_piece(arrays, axis, dim, along):
    both = jnp.concatenate(arrays, axis=along)
    whole, at, done = (sent_and_summed(both, axis, dim), 0, [])
    for a in arrays:
        done.append(lax.slice_in_dim(whole, at, at + a.shape[along], axis=along))
        at += a.shape[along]
    return tuple(done)


def summed_rows(total, axes):
    for axis in axes:
        total = lax.psum_scatter(total, axis, scatter_dimension=0, tiled=True)
    return total


def action_table(actions, count):
    return (actions[:, None] == jnp.arange(count, dtype=jnp.int32)[None, :]).astype(jnp.float32)


def picked_rows(indices, hot):
    chosen = jnp.sum(jnp.where(hot[:, :, None] > 0, indices, 0), axis=1)
    return chosen.T


def body(alpha_set, transitions, obs_weights, rewards, chosen_idx, chosen_action):
    actions = rewards.shape[0]
    states = rewards.shape[1]
    obs_local = obs_weights.shape[0]
    bel_rows = chosen_action.shape[0]
    trans_raw = transitions.astype(jnp.float32)
    action_hot = action_table(chosen_action, actions)
    picks = picked_rows(chosen_idx, action_hot).reshape(-1)
    piece = lax.all_gather(alpha_set, "bel", axis=0, tiled=True)
    count = piece.shape[0]
    onehot = (picks[:, None] == jnp.arange(count, dtype=jnp.int32)[None, :]).astype(jnp.bfloat16)
    chosen = jnp.dot(onehot, piece, preferred_element_type=jnp.float32)
    chosen = chosen.reshape(obs_local, bel_rows, states)
    trans_totals = over_pieces(jnp.sum(trans_raw, axis=1), OBS)
    belief_raw = jnp.einsum("ba,oas->obs", action_hot, obs_weights, precision=lax.Precision.HIGHEST)
    partial_value = jnp.sum(belief_raw * chosen, axis=0)
    raw_slice, total_slice = in_one_piece((partial_value, jnp.sum(obs_weights, axis=0)), OBS, 1, 0)
    divisor = jnp.dot(
        action_hot, total_slice, precision=lax.Precision.HIGHEST, preferred_element_type=jnp.float32
    )
    slice_w = raw_slice / divisor
    trans_prob = trans_raw / trans_totals[:, None, :]
    width = slice_w.shape[1]
    spread = (action_hot[:, :, None] * slice_w[:, None, :]).reshape(bel_rows, actions * width)
    table = trans_prob.reshape(actions * width, states)
    owned = bel_rows // lax.axis_size(OBS)
    future = summed_rows(
        jnp.dot(spread, table, precision=lax.Precision.HIGHEST, preferred_element_type=jnp.float32),
        OBS,
    )
    own_hot = lax.dynamic_slice_in_dim(action_hot, lax.axis_index(OBS) * owned, owned, 0)
    reward_rows = jnp.dot(
        own_hot, rewards, precision=lax.Precision.HIGHEST, preferred_element_type=jnp.float32
    )
    return reward_rows + discount * future


def solution(mesh):
    torus = Mesh(
        mesh.devices.reshape(8, 4, 2, mesh.shape["bel"]), ("obs_0", "obs_1", "obs_2", "bel")
    )
    return jax.shard_map(
        body,
        mesh=torus,
        in_specs=(
            P("bel", None),
            P(None, OBS, None),
            P(OBS, None, None),
            P(),
            P("bel", None, OBS),
            P("bel"),
        ),
        out_specs=P(BEL_OBS, None),
        check_vma=False,
    )
```

profile of v0, /device:TPU:1, one launch (start us, length us, event | category | flops | bytes accessed | tf_op | source)
XLA Modules:
  0.0 339.2 jit_solution(6894292700432248793)
XLA Ops:
  6.5 0.0 all-gather.4.cloned.1.call-start
  6.6 0.7 all-gather.4.cloned.1.call-update
  7.3 0.0 all-gather.6.cloned.1.call-start
  7.3 2.8 convert_reduce_fusion
  10.1 0.0 all-gather.6.cloned.1.call-update
  10.1 0.6 iota_compare_fusion.2
  10.8 0.1 select_reduce_fusion
  10.9 87.6 %all-gather.4.cloned.1.call-done = bf16[2048,2048]{1,0:T(8,128)(2,1)} async-done(((bf16[512,2048]{1,0:T(8,128)(2,1)}), bf16[2048,2048]{1,0:T(8,128)(2,1)}) %all-gather.4.cloned.1.call-update) | async-done | bytes 8388624 | tf_op jit(solution)/shard_map/all_gather | solution.py:63
  98.5 15.6 %fusion.3 = f32[1536,2048]{1,0:T(8,128)S(1)} fusion(bf16[2048,2048]{1,0:T(8,128)(2,1)} %all-gather.4.cloned.1.call-done, s32[1536]{0:T(1024)S(1)} %eq.38), kind=kOutput, calls=%fused_computation.3 | convolution fusion | flops 12888047616 | bytes 20977664 | tf_op jit(solution)/shard_map/dot_general | solution.py:66
  114.0 7.3 %fusion.2 = f32[384,2048]{1,0:T(8,128)S(1)} fusion(f32[4,384,2048]{2,1,0:T(8,128)S(1)} %bitcast.24, f32[4,16,2048]{2,1,0:T(8,128)S(1)} %copy-done.1, s32[384]{0:T(512)S(1)} %copy-done.5), kind=kOutput, calls=%fused_computation.1 | convolution fusion | flops 609490944 | bytes 16254464 | tf_op jit(solution)/shard_map/ba,oas->obs/dot_general | solution.py:69
  121.4 0.4 pad_maximum_fusion
  121.8 3.4 %copy.8 = f32[400,2048]{0,1:T(8,128)} copy(f32[400,2048]{1,0:T(8,128)S(1)} %pad_maximum_fusion) | data formatting | bytes 6553600 | tf_op jit(solution)/shard_map/concatenate | solution.py:32
  125.2 11.0 %all-to-all-start = ((f32[64,400,32]{1,2,0:T(8,128)}), f32[64,400,32]{1,2,0:T(8,128)}, u32[]{:S(2)}, u32[]{:S(2)}) async-start(f32[64,400,32]{1,2,0:T(8,128)} %bitcast.25), calls=%async_computation | async-start | bytes 8388608 | tf_op jit(solution)/shard_map/all_to_all | solution.py:27
  136.2 0.2 reduce-scatter.6.cloned.1.call-start
  136.4 95.8 %all-gather.6.cloned.1.call-done = f32[1024,2048]{1,0:T(8,128)} async-done(((f32[16,2048]{1,0:T(8,128)}), f32[1024,2048]{1,0:T(8,128)}) %all-gather.6.cloned.1.call-update) | async-done | bytes 8388624 | tf_op jit(solution)/shard_map/all_gather | solution.py:15
  232.2 3.8 %reduce_sum.59 = f32[16,2048]{1,0:T(8,128)S(1)} reduce(f32[64,16,2048]{2,1,0:T(8,128)} %bitcast.26, f32[]{:T(128)} %constant.28.clone.1), dimensions={0}, to_apply=%region_5.6 | reduce | flops 2064384 | bytes 8519684 | tf_op jit(solution)/shard_map/reduce_sum | solution.py:16
  236.0 14.5 %all-to-all-done = f32[64,400,32]{1,2,0:T(8,128)} async-done(((f32[64,400,32]{1,2,0:T(8,128)}), f32[64,400,32]{1,2,0:T(8,128)}, u32[]{:S(2)}, u32[]{:S(2)}) %all-to-all-start) | async-done | bytes 3276832 | tf_op jit(solution)/shard_map/all_to_all | solution.py:27
  250.5 2.5 reduce_sum.57
  253.0 0.2 convolution_divide_fusion
  253.2 7.0 %fusion.6 = f32[384,2048]{1,0:T(8,128)} fusion(bf16[16,32,2048]{2,1,0:T(8,128)(2,1)S(1)} %copy-done.2, f32[16,2048]{1,0:T(8,128)S(1)} %reduce_sum.59, f32[384,32]{0,1:T(8,128)S(1)} %convolution_divide_fusion, f32[384,16]{0,1:T(8,128)S(1)} %copy-done.4), kind=kOutput, calls=%fused_computation.9 | convolution fusion | flops 4834131968 | bytes 5447680 | tf_op jit(solution)/shard_map/dot_general | solution.py:82
  260.2 41.5 %reduce-scatter.6.cloned.1.call-done = f32[48,2048]{1,0:T(8,128)} async-done(((f32[384,2048]{1,0:T(8,128)}), f32[48,2048]{1,0:T(8,128)}) %reduce-scatter.6.cloned.1.call-update) | async-done | bytes 393232 | tf_op jit(solution)/shard_map/reduce_scatter | solution.py:42
  301.7 12.0 %fusion = f32[16,2048]{1,0:T(8,128)S(1)} fusion(f32[48,2048]{1,0:T(8,128)} %reduce-scatter.6.cloned.1.call-done), kind=kCustom, calls=%all-reduce-scatter | all-reduce-scatter fusion | flops 131073 | bytes 525312
  313.8 4.0 %collective-permute-start = (f32[12,2048]{1,0:T(8,128)S(1)}, f32[12,2048]{1,0:T(8,128)S(1)}, u32[]{:S(2)}, u32[]{:S(2)}) collective-permute-start(f32[12,2048]{1,0:T(8,128)S(1)} %slice.10), channel_id=1, source_target_pairs={{0,8},{8,16},{16,24},{1,9},{9,17},{17,25},{2,10},{10,18},{18,26},{... | collective-permute-start | bytes 294920
  317.8 0.6 dynamic-slice.6
  319.0 0.7 collective-permute-done
  319.7 0.2 concatenate.4
  319.9 8.5 %fusion.1 = f32[8,2048]{1,0:T(8,128)S(1)} fusion(f32[12,2048]{1,0:T(8,128)S(1)} %constant_dynamic-slice_fusion), kind=kCustom, calls=%all-reduce-scatter.1 | all-reduce-scatter fusion | flops 32769 | bytes 164864
  328.5 1.3 collective-permute-start.1
  329.8 0.6 dynamic-slice.10
  331.1 0.5 collective-permute-done.1
  331.6 0.1 concatenate.5
  331.7 0.9 fusion.11
  (22 shorter events, 0.1 us)
Async XLA Ops:
  6.5 325.2 %copy-start = (f32[16,2048]{1,0:T(8,128)S(1)}, f32[16,2048]{1,0:T(8,128)}, u32[]{:S(2)}) copy-start(f32[16,2048]{1,0:T(8,128)} %param.9) | copy-start | bytes 393220
  6.5 3.6 %copy-start.5 = (s32[384]{0:T(512)S(1)}, s32[384]{0:T(512)}, u32[]{:S(2)}) copy-start(s32[384]{0:T(512)} %param.11) | copy-start | bytes 4612
  6.5 4.2 %copy-start.3 = (s32[384,16,4]{0,2,1:T(4,128)S(1)}, s32[384,16,4]{0,2,1:T(4,128)}, u32[]{:S(2)}) copy-start(s32[384,16,4]{0,2,1:T(4,128)} %param.10) | copy-start | bytes 294916
  6.5 4.3 %copy-start.1 = (f32[4,16,2048]{2,1,0:T(8,128)S(1)}, f32[4,16,2048]{2,1,0:T(8,128)}, u32[]{:S(2)}) copy-start(f32[4,16,2048]{2,1,0:T(8,128)} %param.8) | copy-start | bytes 1572868
  6.5 91.9 %all-gather.4.cloned.1.call-start = ((), (), s32[]{:S(2)}) async-start(), calls=%async_computation.2 | async-start | bytes 10485760 | tf_op jit(solution)/shard_map/all_gather | solution.py:63
  7.3 224.9 %all-gather.6.cloned.1.call-start = ((), (), s32[]{:S(2)}) async-start(), calls=%async_computation.4 | async-start | bytes 8519680 | tf_op jit(solution)/shard_map/all_gather | solution.py:15
  125.2 125.4 %all-to-all-start = ((f32[64,400,32]{1,2,0:T(8,128)}), f32[64,400,32]{1,2,0:T(8,128)}, u32[]{:S(2)}, u32[]{:S(2)}) async-start(f32[64,400,32]{1,2,0:T(8,128)} %bitcast.25), calls=%async_computation | async-start | bytes 8388608 | tf_op jit(solution)/shard_map/all_to_all | solution.py:27
  136.2 165.6 %reduce-scatter.6.cloned.1.call-start = ((), (), s32[]{:S(2)}) async-start(), calls=%async_computation.3 | async-start | bytes 3538944 | tf_op jit(solution)/shard_map/reduce_scatter | solution.py:42
  236.0 17.2 %copy-start.2 = (bf16[16,32,2048]{2,1,0:T(8,128)(2,1)S(1)}, bf16[16,32,2048]{2,1,0:T(8,128)(2,1)}, u32[]{:S(2)}) copy-start(bf16[16,32,2048]{2,1,0:T(8,128)(2,1)} %param.7) | copy-start | bytes 6291460
  236.0 17.2 %copy-start.4 = (f32[384,16]{0,1:T(8,128)S(1)}, f32[384,16]{0,1:T(8,128)}, u32[]{:S(2)}) copy-start(f32[384,16]{0,1:T(8,128)} %get-tuple-element.7) | copy-start | bytes 73732
  253.2 64.6 %copy-start.7 = (u32[256]{0:T(256)S(1)}, u32[256]{0:T(256)}, u32[]{:S(2)}) copy-start(u32[256]{0:T(256)} %constant.35) | copy-start | bytes 3076
  260.2 69.6 %copy-start.6 = (u32[256]{0:T(256)S(1)}, u32[256]{0:T(256)}, u32[]{:S(2)}) copy-start(u32[256]{0:T(256)} %constant.39) | copy-start | bytes 3076
  313.8 5.9 %collective-permute-start = (f32[12,2048]{1,0:T(8,128)S(1)}, f32[12,2048]{1,0:T(8,128)S(1)}, u32[]{:S(2)}, u32[]{:S(2)}) collective-permute-start(f32[12,2048]{1,0:T(8,128)S(1)} %slice.10), channel_id=1, source_target_pairs={{0,8},{8,16},{16,24},{1,9},{9,17},{17,25},{2,10},{10,18},{18,26},{... | collective-permute-start | bytes 294920
  328.5 3.1 collective-permute-start.1
Sparse Core Ops, SparseCore 0:
  9.2 89.2 all-gather.3
  101.2 130.9 all-gather.5
  260.4 41.3 reduce-scatter.5
where the time goes:
time: 340 us; the launch traced here: 339 us
  waiting for transfers between devices  241 us (71%)
  matrix products  31 us (9%)
  blocking collectives  20.5 us (6%)
  starting transfers between devices  16.6 us (5%)
  between operations  14.6 us (4%)
  other arithmetic  10.1 us (3%)
  local copies, waits for them, and re-layouts  5 us (1%)
    all_gather x1, waiting for transfers between devices, over_pieces(): blocks = lax.all_gather(x, axis)  95.8 us
    all_gather x1, waiting for transfers between devices, body(): piece = lax.all_gather(alpha_set, 'bel', axis=0, tiled=True)  87.6 us
    reduce_scatter x1, waiting for transfers between devices, summed_rows(): total = lax.psum_scatter(total, axis, scatter_dimension=0, tiled=True)  41.5 us
    unnamed x2, blocking collectives  20.5 us
    dot_general x1, matrix products, body(): chosen = jnp.dot(onehot, piece, preferred_element_type=jnp.float32)  15.6 us
    all_to_all x1, waiting for transfers between devices, sent_and_summed(): lax.all_to_all(blocks, axis, split_axis=0, concat_axis=0, tiled=True)  14.5 us
    all_to_all x1, starting transfers between devices, sent_and_summed(): lax.all_to_all(blocks, axis, split_axis=0, concat_axis=0, tiled=True)  11 us
    dot_general x1, matrix products, body(): jnp.einsum('ba,oas->obs', action_hot, obs_weights, precision=lax.Precisio...  7.34 us
  transfers between devices with their start and end apart: 6, of which 6 were waited for; matrix products, arithmetic and copies ran while one was open for 10% of the time, Pallas kernels for 0%

commit v1 on v0

v1 whole, which is shorter than its diff:
```python
import functools

import jax
import jax.numpy as jnp
from jax import lax
from jax.experimental import pallas as pl
from jax.experimental.pallas import tpu as pltpu
from jax.sharding import Mesh
from jax.sharding import PartitionSpec as P

OBS = ("obs_0", "obs_1", "obs_2")
BEL_OBS = ("bel", "obs_0", "obs_1", "obs_2")
LANES = 128
DISCOUNT = 0.95
MESH = pl.DeviceIdType.MESH


def kernel(
    dims,
    act_s,
    picks_hbm,
    act_i,
    act_b,
    alpha_hbm,
    trans_hbm,
    obs_hbm,
    rew_hbm,
    out_ref,
    al_bf,
    al_rows,
    obs_all,
    obs_rows,
    pk_v,
    pk_s,
    part,
    rs_buf,
    tot_own,
    tot_buf,
    w_all,
    t_blk,
    spread,
    fut,
    f_buf,
    tt_own,
    tt_buf,
    rew_v,
    fin,
    local_sem,
    pk_send,
    pk_recv,
    al_send,
    al_recv,
    ob_send,
    ob_recv,
    t_send,
    t_recv,
    tot_send,
    tot_recv,
    rs_send,
    rs_recv,
    w_send,
    w_recv,
    f_send,
    f_recv,
    tt_send,
    tt_recv,
    o_send,
    o_recv,
):
    ny, nz, nx, nc = dims
    ng = nx * nc
    actions = t_blk.shape[0]
    width = t_blk.shape[1]
    qwidth = t_blk.shape[2]
    halves = width // LANES
    bel = fut.shape[0]
    own_rows = bel // ng
    z_rows = bel // nz
    rows_y = alpha_hbm.shape[0]
    obs_local = obs_hbm.shape[0]
    t_rows = trans_hbm.shape[1]
    pk_len = picks_hbm.shape[0]
    pk_pitch = pk_len // obs_local
    last = fin.shape[1]

    y = lax.axis_index("bel")
    z = lax.axis_index("obs_0")
    x = lax.axis_index("obs_1")
    c = lax.axis_index("obs_2")
    g = x * nc + c

    def y_at(t):
        return lax.rem(y + 1 + t, ny)

    def z_at(t):
        return lax.rem(z + 1 + t, nz)

    def g_at(t):
        return lax.rem(g + 1 + t, ng)

    def to_y(t):
        return {"bel": y_at(t)}

    def to_z(t):
        return {"obs_0": z_at(t)}

    def to_g(t):
        j = g_at(t)
        return {"obs_1": j // nc, "obs_2": lax.rem(j, nc)}

    peers = (
        [to_y(t) for t in range(ny - 1)]
        + [to_z(t) for t in range(nz - 1)]
        + [to_g(t) for t in range(ng - 1)]
    )
    barrier = pltpu.get_barrier_semaphore()
    for peer in peers:
        pl.semaphore_signal(barrier, inc=1, device_id=peer, device_id_type=MESH)

    z_cols = pl.ds(pl.multiple_of(z * width, width), width)
    q_cols = pl.ds(pl.multiple_of(g * qwidth, qwidth), qwidth)

    own_pk = pltpu.make_async_copy(
        picks_hbm, pk_v.at[pl.ds(pl.multiple_of(z * pk_len, pk_len), pk_len)], local_sem.at[0]
    )
    own_al = pltpu.make_async_copy(alpha_hbm.at[:, z_cols], al_bf.at[y], local_sem.at[1])
    own_ob = pltpu.make_async_copy(obs_hbm.at[:, :, z_cols], obs_all.at[z], local_sem.at[2])
    own_t = pltpu.make_async_copy(
        trans_hbm.at[:, :, q_cols],
        t_blk.at[:, pl.ds(pl.multiple_of(g * t_rows, t_rows), t_rows), :],
        local_sem.at[3],
    )
    own_rew = pltpu.make_async_copy(rew_hbm.at[:, q_cols], rew_v, local_sem.at[4])
    own_al.start()
    own_ob.start()
    own_pk.start()
    own_t.start()
    own_rew.start()
    pl.semaphore_wait(barrier, len(peers))

    pk_cp = [
        pltpu.make_async_remote_copy(
            picks_hbm,
            pk_v.at[pl.ds(pl.multiple_of(z * pk_len, pk_len), pk_len)],
            pk_send.at[t],
            pk_recv.at[t],
            device_id=to_z(t),
            device_id_type=MESH,
        )
        for t in range(nz - 1)
    ]
    al_cp = [
        pltpu.make_async_remote_copy(
            alpha_hbm.at[:, z_cols],
            al_bf.at[y],
            al_send.at[t],
            al_recv.at[t],
            device_id=to_y(t),
            device_id_type=MESH,
        )
        for t in range(ny - 1)
    ]
    ob_cp = [
        pltpu.make_async_remote_copy(
            obs_hbm.at[:, :, pl.ds(pl.multiple_of(z_at(t) * width, width), width)],
            obs_all.at[z],
            ob_send.at[t],
            ob_recv.at[t],
            device_id=to_z(t),
            device_id_type=MESH,
        )
        for t in range(nz - 1)
    ]
    t_cp = [
        pltpu.make_async_remote_copy(
            trans_hbm.at[:, :, pl.ds(pl.multiple_of(g_at(t) * qwidth, qwidth), qwidth)],
            t_blk.at[:, pl.ds(pl.multiple_of(g * t_rows, t_rows), t_rows), :],
            t_send.at[t],
            t_recv.at[t],
            device_id=to_g(t),
            device_id_type=MESH,
        )
        for t in range(ng - 1)
    ]
    for cp in pk_cp:
        cp.start()
    for cp in al_cp:
        cp.start()
    for cp in ob_cp:
        cp.start()
    for cp in t_cp:
        cp.start()

    def spread_alpha(block):
        def rows16(n, carry):
            r = pl.multiple_of(n * 16, 16)
            v = al_bf[block, pl.ds(r, 16), :].astype(jnp.float32)
            for h in range(halves):
                al_rows[pl.ds(block * rows_y + r, 16), h, :] = v[:, h * LANES : (h + 1) * LANES]
            return carry

        lax.fori_loop(0, rows_y // 16, rows16, 0, unroll=4)

    own_al.wait()
    spread_alpha(y)

    own_pk.wait()
    for cp in pk_cp:
        cp.wait_recv()
    to_scalar = pltpu.make_async_copy(pk_v, pk_s, local_sem.at[5])
    to_scalar.start()

    own_ob.wait()
    for cp in ob_cp:
        cp.wait_recv()
    totals = [jnp.zeros((actions, LANES), jnp.float32) for _ in range(halves)]
    for s in range(nz):
        for o in range(obs_local):
            for h in range(halves):
                v = obs_all[s, o, :, h * LANES : (h + 1) * LANES]
                totals[h] = totals[h] + v
                first = (s * obs_local + o) * actions
                obs_rows[first : first + actions, h, :] = v
    for h in range(halves):
        tot_own[h] = totals[h]
    tot_cp = [
        pltpu.make_async_remote_copy(
            tot_own, tot_buf.at[t], tot_send.at[t], tot_recv.at[t], device_id=to_g(t), device_id_type=MESH
        )
        for t in range(ng - 1)
    ]
    for cp in tot_cp:
        cp.start()

    for t in range(ny - 1):
        al_cp[t].wait_recv()
        spread_alpha(lax.rem(y + ny - 1 - t, ny))

    to_scalar.wait()
    rs_cp = []
    for t in range(ng):
        j = g_at(t)

        def one_belief(r, carry):
            b = j * own_rows + r
            a = act_s[b]
            sums = [None] * 4
            n = 0
            for s in range(nz):
                for o in range(obs_local):
                    k = pk_s[s * pk_len + o * pk_pitch + b]
                    rows = al_rows[k]
                    probs = obs_rows[(s * obs_local + o) * actions + a]
                    term = rows * probs
                    sums[n % 4] = term if sums[n % 4] is None else sums[n % 4] + term
                    n += 1
            part[pl.ds(pl.multiple_of(b * halves, halves), halves), :] = (sums[0] + sums[1]) + (
                sums[2] + sums[3]
            )
            return carry

        lax.fori_loop(0, own_rows, one_belief, 0)
        if t < ng - 1:
            rows = own_rows * halves
            cp = pltpu.make_async_remote_copy(
                part.at[pl.ds(pl.multiple_of(j * rows, rows), rows), :],
                rs_buf.at[t],
                rs_send.at[t],
                rs_recv.at[t],
                device_id=to_g(t),
                device_id_type=MESH,
            )
            cp.start()
            rs_cp.append(cp)

    for cp in tot_cp:
        cp.wait_recv()
    for cp in rs_cp:
        cp.wait_recv()
    act_own = act_i[pl.ds(pl.multiple_of(g * own_rows, own_rows), own_rows), :]
    for h in range(halves):
        total = tot_own[h]
        for t in range(ng - 1):
            total = total + tot_buf[t, h]
        raw = part[pl.ds(g * own_rows * halves + h, own_rows, stride=halves), :]
        for t in range(ng - 1):
            raw = raw + rs_buf[t, pl.ds(h, own_rows, stride=halves), :]
        divisor = jnp.ones((own_rows, LANES), jnp.float32)
        for a in range(actions):
            divisor = jnp.where(act_own == a, total[a : a + 1, :], divisor)
        w = raw / divisor
        hi = w.astype(jnp.bfloat16)
        lo = (w - hi.astype(jnp.float32)).astype(jnp.bfloat16)
        w_all[g, 0, :, h * LANES : (h + 1) * LANES] = hi
        w_all[g, 1, :, h * LANES : (h + 1) * LANES] = lo

    w_cp = [
        pltpu.make_async_remote_copy(
            w_all.at[g], w_all.at[g], w_send.at[t], w_recv.at[t], device_id=to_g(t), device_id_type=MESH
        )
        for t in range(ng - 1)
    ]
    for cp in w_cp:
        cp.start()
    for cp in w_cp:
        cp.wait_recv()

    def spread_action(a, carry):
        hot = act_b[...] == a.astype(jnp.bfloat16)
        for k in range(2):
            for h in range(halves):
                val = w_all[:, k, :, h * LANES : (h + 1) * LANES].reshape(bel, LANES)
                spread[
                    k * bel : (k + 1) * bel,
                    pl.ds(pl.multiple_of(a * width + h * LANES, LANES), LANES),
                ] = jnp.where(hot, val, jnp.zeros_like(val))
        return carry

    lax.fori_loop(0, actions, spread_action, 0)

    own_t.wait()
    for cp in t_cp:
        cp.wait_recv()
    both = jnp.dot(
        spread[...],
        t_blk[...].reshape(actions * width, qwidth),
        preferred_element_type=jnp.float32,
    )
    fut[...] = both[:bel] + both[bel:]
    f_cp = [
        pltpu.make_async_remote_copy(
            fut.at[pl.ds(pl.multiple_of(z_at(t) * z_rows, z_rows), z_rows), :],
            f_buf.at[t],
            f_send.at[t],
            f_recv.at[t],
            device_id=to_z(t),
            device_id_type=MESH,
        )
        for t in range(nz - 1)
    ]
    for cp in f_cp:
        cp.start()

    def total_action(a, carry):
        tt_own[pl.ds(a, 1), :] = jnp.sum(
            t_blk[a].astype(jnp.float32), axis=0, keepdims=True
        )
        return carry

    lax.fori_loop(0, actions, total_action, 0)
    tt_cp = [
        pltpu.make_async_remote_copy(
            tt_own, tt_buf.at[t], tt_send.at[t], tt_recv.at[t], device_id=to_z(t), device_id_type=MESH
        )
        for t in range(nz - 1)
    ]
    for cp in tt_cp:
        cp.start()
    own_rew.wait()
    for cp in f_cp:
        cp.wait_recv()
    for cp in tt_cp:
        cp.wait_recv()
    z_start = pl.multiple_of(z * z_rows, z_rows)
    act_z = act_i[pl.ds(z_start, z_rows), :]
    for h in range(qwidth // LANES):
        cols = slice(h * LANES, (h + 1) * LANES)
        total = tt_own[:, cols]
        for t in range(nz - 1):
            total = total + tt_buf[t, :, cols]
        future = fut[pl.ds(z_start, z_rows), cols]
        for t in range(nz - 1):
            future = future + f_buf[t, :, cols]
        divisor = jnp.ones((z_rows, LANES), jnp.float32)
        reward = jnp.zeros((z_rows, LANES), jnp.float32)
        for a in range(actions):
            hot = act_z == a
            divisor = jnp.where(hot, total[a : a + 1, :], divisor)
            reward = jnp.where(hot, rew_v[a : a + 1, cols], reward)
        result = reward + DISCOUNT * (future / divisor)
        for n in range(ng):
            fin[n, :, cols] = result[n * last : (n + 1) * last, :]
    o_cp = [
        pltpu.make_async_remote_copy(
            fin.at[g_at(t)],
            out_ref.at[:, q_cols],
            o_send.at[t],
            o_recv.at[t],
            device_id=to_g(t),
            device_id_type=MESH,
        )
        for t in range(ng - 1)
    ]
    for cp in o_cp:
        cp.start()
    out_ref[:, q_cols] = fin[g]
    for cp in o_cp:
        cp.wait_recv()
    for cp in ob_cp + pk_cp + al_cp + t_cp + tot_cp + rs_cp + w_cp + f_cp + tt_cp + o_cp:
        cp.wait_send()


def body(dims, alpha_set, transitions, obs_weights, rewards, chosen_idx, chosen_action):
    ny, nz, nx, nc = dims
    ng = nx * nc
    actions, states = rewards.shape
    bel = chosen_action.shape[0]
    obs_local = obs_weights.shape[0]
    width = states // nz
    qwidth = states // ng
    halves = width // LANES
    count = alpha_set.shape[0] * ny
    hot = chosen_action[:, None] == jnp.arange(actions, dtype=jnp.int32)[None, :]
    picks = jnp.sum(jnp.where(hot[:, :, None], chosen_idx, 0), axis=1).T
    pitch = -(-bel // 256) * 256
    picks = jnp.pad(picks, ((0, 0), (0, pitch - bel))).reshape(-1)
    act_i = jnp.broadcast_to(chosen_action[:, None], (bel, LANES))
    act_b = act_i.astype(jnp.bfloat16)
    f32, b16, i32 = jnp.float32, jnp.bfloat16, jnp.int32
    dma = pltpu.SemaphoreType.DMA
    vmem = pl.BlockSpec(memory_space=pltpu.VMEM)
    hbm = pl.BlockSpec(memory_space=pl.ANY)
    z_rows = bel // nz
    own_rows = bel // ng
    scratch = [
        pltpu.VMEM((ny, count // ny, width), b16),
        pltpu.VMEM((count, halves, LANES), f32),
        pltpu.VMEM((nz, obs_local, actions, width), f32),
        pltpu.VMEM((nz * obs_local * actions, halves, LANES), f32),
        pltpu.VMEM((nz * obs_local * pitch,), i32),
        pltpu.SMEM((nz * obs_local * pitch,), i32),
        pltpu.VMEM((bel * halves, LANES), f32),
        pltpu.VMEM((ng - 1, own_rows * halves, LANES), f32),
        pltpu.VMEM((halves, actions, LANES), f32),
        pltpu.VMEM((ng - 1, halves, actions, LANES), f32),
        pltpu.VMEM((ng, 2, own_rows, width), b16),
        pltpu.VMEM((actions, width, qwidth), b16),
        pltpu.VMEM((2 * bel, actions * width), b16),
        pltpu.VMEM((bel, qwidth), f32),
        pltpu.VMEM((nz - 1, z_rows, qwidth), f32),
        pltpu.VMEM((actions, qwidth), f32),
        pltpu.VMEM((nz - 1, actions, qwidth), f32),
        pltpu.VMEM((actions, qwidth), f32),
        pltpu.VMEM((ng, bel // (nz * ng), qwidth), f32),
        dma((6,)),
        dma((nz - 1,)),
        dma((nz - 1,)),
        dma((ny - 1,)),
        dma((ny - 1,)),
        dma((nz - 1,)),
        dma((nz - 1,)),
        dma((ng - 1,)),
        dma((ng - 1,)),
        dma((ng - 1,)),
        dma((ng - 1,)),
        dma((ng - 1,)),
        dma((ng - 1,)),
        dma((ng - 1,)),
        dma((ng - 1,)),
        dma((nz - 1,)),
        dma((nz - 1,)),
        dma((nz - 1,)),
        dma((nz - 1,)),
        dma((ng - 1,)),
        dma((ng - 1,)),
    ]
    return pl.pallas_call(
        functools.partial(kernel, dims),
        out_shape=jax.ShapeDtypeStruct((bel // (nz * ng), states), f32),
        in_specs=[
            pl.BlockSpec(memory_space=pltpu.SMEM),
            hbm,
            vmem,
            vmem,
            hbm,
            hbm,
            hbm,
            hbm,
        ],
        out_specs=vmem,
        scratch_shapes=scratch,
        compiler_params=pltpu.CompilerParams(
            collective_id=0, has_side_effects=True, vmem_limit_bytes=60 * 1024 * 1024
        ),
        name="backup",
    )(chosen_action, picks, act_i, act_b, alpha_set, transitions, obs_weights, rewards)


def solution(mesh):
    dims = (mesh.shape["bel"], 8, 4, 2)
    torus = Mesh(
        mesh.devices.reshape(*dims[1:], dims[0]), ("obs_0", "obs_1", "obs_2", "bel")
    )
    return jax.shard_map(
        functools.partial(body, dims),
        mesh=torus,
        in_specs=(
            P("bel", None),
            P(None, OBS, None),
            P(OBS, None, None),
            P(),
            P("bel", None, OBS),
            P("bel"),
        ),
        out_specs=P(BEL_OBS, None),
        check_vma=False,
    )
```

time: 340 us -> 86.3 us (0.25)
  waiting for transfers between devices: 241 us -> 0 us
  Pallas kernels: 0 us -> 79.4 us
  matrix products: 31 us -> 0 us
  blocking collectives: 20.5 us -> 0 us
  starting transfers between devices: 16.6 us -> 0 us
  between operations: 14.6 us -> 0.01 us
  other arithmetic: 10.1 us -> 2.31 us
    all_gather x2 -> x0, waiting for transfers between devices: 183 us -> none  [the longest x1 95.8 us: over_pieces(): blocks = lax.all_gather(x, axis)]
    pallas_call x0 -> x1, Pallas kernels: none -> 79.4 us  [body(): pl.pallas_call(functools.partial(kernel, dims), out_shape=jax.ShapeDtypeS...]
    reduce_scatter x1 -> x0, waiting for transfers between devices: 41.5 us -> none  [summed_rows(): total = lax.psum_scatter(total, axis, scatter_dimension=0, tiled=True)]
    dot_general x5 -> x0, matrix products: 31 us -> none  [the longest x1 15.6 us: body(): chosen = jnp.dot(onehot, piece, preferred_element_type=jnp.float32)]
    unnamed x2 -> x0, blocking collectives: 20.5 us -> none
    all_to_all x1 -> x0, waiting for transfers between devices: 14.5 us -> none  [sent_and_summed(): lax.all_to_all(blocks, axis, split_axis=0, concat_axis=0, tiled=True)]
    all_to_all x1 -> x0, starting transfers between devices: 11 us -> none  [sent_and_summed(): lax.all_to_all(blocks, axis, split_axis=0, concat_axis=0, tiled=True)]
    reduce_sum x5 -> x1, other arithmetic: 9.15 us -> 0.94 us  [body(): picks = jnp.sum(jnp.where(hot[:, :, None], chosen_idx, 0), axis=1).T]
  transfers between devices with their start and end apart: 6 -> 0, of which waited for: 6 -> 0; matrix products, arithmetic and copies ran while one was open for 10% -> 0% of each run, Pallas kernels for 0% -> 0%
where the time goes in v1:
time: 86.3 us; the launch traced here: 86 us
  Pallas kernels  79.4 us (92%)
  local copies, waits for them, and re-layouts  4.3 us (5%)
  other arithmetic  2.31 us (3%)
    pallas_call x1, Pallas kernels, body(): pl.pallas_call(functools.partial(kernel, dims), out_shape=jax.ShapeDtypeS...  79.4 us
    broadcast_in_dim x2, local copies, waits for them, and re-layouts, body(): act_i = jnp.broadcast_to(chosen_action[:, None], (bel, LANES))  2.22 us
    unnamed x3, local copies, waits for them, and re-layouts  2.08 us

profile of v1, /device:TPU:1, one launch (start us, length us, event | category | flops | bytes accessed | tf_op | source)
XLA Modules:
  0.0 86.0 jit_solution(10177613932357052363)
XLA Ops:
  0.0 0.7 convert_element_type.3
  0.7 0.7 iota_compare_fusion
  1.4 0.9 %select_reduce_fusion = s32[384,4]{0,1:T(4,128)S(1)} fusion(s32[384,16,4]{0,2,1:T(4,128)} %param.10, pred[384,16]{0,1:T(8,128)(4,1)S(1)} %iota_compare_fusion), kind=kLoop, calls=%fused_computation | loop fusion | flops 47616 | bytes 110592 | tf_op jit(solution)/shard_map/reduce_sum | solution.py:414
  2.3 0.6 copy.7
  2.9 0.8 broadcast_in_dim.26.act_b
  3.7 1.5 %broadcast_in_dim.25.act_i = s32[384,128]{1,0:T(8,128)} broadcast(s32[384]{0:T(512)} %act_s.1), dimensions={0} | broadcast | bytes 198144 | tf_op jit(solution)/shard_map/broadcast_in_dim | solution.py:417
  5.1 79.4 %backup.1 = f32[6,2048]{1,0:T(8,128)} custom-call(s32[384]{0:T(512)} %act_s.1, s32[2048]{0:T(1024)} %bitcast.4, s32[384,128]{1,0:T(8,128)} %broadcast_in_dim.25.act_i, bf16[384,128]{1,0:T(8,128)(2,1)} %broadcast_in_dim.26.act_b, bf16[512,2048]{1,0:T(8,128)(2,1)} %alpha_hbm.1, bf16[16,32,2048]{2,1,0:T(8,128)(2,1)} %trans_hbm.1, f32[4,16,2048]{2,1,0:T(8,128)} %obs_hbm.1, ...), custom_call_target="tpu_custom_call" | custom-call | tf_op jit(solution)/shard_map/backup/pallas_call | solution.py:467
  84.5 1.5 %copy.9 = f32[6,2048]{1,0:T(8,128)} copy(f32[6,2048]{1,0:T(8,128)} %backup.1) | data formatting | bytes 98304
  (1 shorter events, 0.0 us)

commit v2 on v1

--- a/solution.py
+++ b/solution.py
@@ -12,15 +12,16 @@
 BEL_OBS = ("bel", "obs_0", "obs_1", "obs_2")
 LANES = 128
 DISCOUNT = 0.95
+CODE_SCALE = 14114.0
+CODE_SHIFT = 2.302585093 * CODE_SCALE
 MESH = pl.DeviceIdType.MESH
 
 
 def kernel(
     dims,
     act_s,
-    picks_hbm,
-    act_i,
-    act_b,
+    act_row,
+    idx_ref,
     alpha_hbm,
     trans_hbm,
     obs_hbm,
@@ -28,8 +29,13 @@
     out_ref,
     al_bf,
     al_rows,
+    act_i,
+    act_b,
+    obs_v,
+    obs_code,
     obs_all,
     obs_rows,
+    pk_own,
     pk_v,
     pk_s,
     part,
@@ -50,6 +56,8 @@
     pk_recv,
     al_send,
     al_recv,
+    al2_send,
+    al2_recv,
     ob_send,
     ob_recv,
     t_send,
@@ -77,10 +85,9 @@
     own_rows = bel // ng
     z_rows = bel // nz
     rows_y = alpha_hbm.shape[0]
+    half_y = rows_y // nc
     obs_local = obs_hbm.shape[0]
     t_rows = trans_hbm.shape[1]
-    pk_len = picks_hbm.shape[0]
-    pk_pitch = pk_len // obs_local
     last = fin.shape[1]
 
     y = lax.axis_index("bel")
@@ -120,28 +127,44 @@
     z_cols = pl.ds(pl.multiple_of(z * width, width), width)
     q_cols = pl.ds(pl.multiple_of(g * qwidth, qwidth), qwidth)
 
-    own_pk = pltpu.make_async_copy(
-        picks_hbm, pk_v.at[pl.ds(pl.multiple_of(z * pk_len, pk_len), pk_len)], local_sem.at[0]
-    )
     own_al = pltpu.make_async_copy(alpha_hbm.at[:, z_cols], al_bf.at[y], local_sem.at[1])
-    own_ob = pltpu.make_async_copy(obs_hbm.at[:, :, z_cols], obs_all.at[z], local_sem.at[2])
+    own_ob = pltpu.make_async_copy(obs_hbm, obs_v, local_sem.at[2])
     own_t = pltpu.make_async_copy(
         trans_hbm.at[:, :, q_cols],
         t_blk.at[:, pl.ds(pl.multiple_of(g * t_rows, t_rows), t_rows), :],
         local_sem.at[3],
     )
     own_rew = pltpu.make_async_copy(rew_hbm.at[:, q_cols], rew_v, local_sem.at[4])
+    own_ob.start()
     own_al.start()
-    own_ob.start()
-    own_pk.start()
     own_t.start()
     own_rew.start()
+
+    picks = jnp.zeros((obs_local, bel), jnp.int32)
+    for a in range(actions):
+        picks = jnp.where(act_row[...] == a, idx_ref[a], picks)
+    for o in range(obs_local):
+        pk_own[o] = picks[o : o + 1, :]
+        pk_v[z, o] = picks[o : o + 1, :]
+
+    def fill_action(b, carry):
+        act_i[pl.ds(b, 1), :] = jnp.full((1, LANES), act_s[b], jnp.int32)
+        return carry
+
+    lax.fori_loop(0, bel, fill_action, 0, unroll=8)
+    act_b[...] = act_i[...].astype(jnp.float32).astype(jnp.bfloat16)
+    own_ob.wait()
+    for n in range(nz):
+        for o in range(obs_local):
+            v = jnp.log(obs_v[o, :, n * width : (n + 1) * width])
+            obs_code[n, o] = jnp.round(v * CODE_SCALE + CODE_SHIFT).astype(jnp.int32).astype(jnp.int16)
     pl.semaphore_wait(barrier, len(peers))
 
+    c_rows = pl.ds(pl.multiple_of(c * half_y, half_y), half_y)
     pk_cp = [
         pltpu.make_async_remote_copy(
-            picks_hbm,
-            pk_v.at[pl.ds(pl.multiple_of(z * pk_len, pk_len), pk_len)],
+            pk_own,
+            pk_v.at[z],
             pk_send.at[t],
             pk_recv.at[t],
             device_id=to_z(t),
@@ -151,8 +174,8 @@
     ]
     al_cp = [
         pltpu.make_async_remote_copy(
-            alpha_hbm.at[:, z_cols],
-            al_bf.at[y],
+            alpha_hbm.at[c_rows, z_cols],
+            al_bf.at[y, c_rows],
             al_send.at[t],
             al_recv.at[t],
             device_id=to_y(t),
@@ -162,7 +185,7 @@
     ]
     ob_cp = [
         pltpu.make_async_remote_copy(
-            obs_hbm.at[:, :, pl.ds(pl.multiple_of(z_at(t) * width, width), width)],
+            obs_code.at[z_at(t)],
             obs_all.at[z],
             ob_send.at[t],
             ob_recv.at[t],
@@ -191,36 +214,44 @@
     for cp in t_cp:
         cp.start()
 
-    def spread_alpha(block):
+    def spread_alpha(block, start, rows):
         def rows16(n, carry):
-            r = pl.multiple_of(n * 16, 16)
+            r = pl.multiple_of(start + n * 16, 16)
             v = al_bf[block, pl.ds(r, 16), :].astype(jnp.float32)
             for h in range(halves):
                 al_rows[pl.ds(block * rows_y + r, 16), h, :] = v[:, h * LANES : (h + 1) * LANES]
             return carry
 
-        lax.fori_loop(0, rows_y // 16, rows16, 0, unroll=4)
+        lax.fori_loop(0, rows // 16, rows16, 0, unroll=4)
 
     own_al.wait()
-    spread_alpha(y)
-
-    own_pk.wait()
+    spread_alpha(y, 0, rows_y)
+
     for cp in pk_cp:
         cp.wait_recv()
-    to_scalar = pltpu.make_async_copy(pk_v, pk_s, local_sem.at[5])
-    to_scalar.start()
-
-    own_ob.wait()
+    to_scalar = [
+        [
+            pltpu.make_async_copy(pk_v.at[n, o], pk_s[n][o], local_sem.at[5 + n * obs_local + o])
+            for o in range(obs_local)
+        ]
+        for n in range(nz)
+    ]
+    for pair in to_scalar:
+        for cp in pair:
+            cp.start()
+
+    for o in range(obs_local):
+        obs_all[z, o] = obs_code[z, o]
     for cp in ob_cp:
         cp.wait_recv()
     totals = [jnp.zeros((actions, LANES), jnp.float32) for _ in range(halves)]
     for s in range(nz):
         for o in range(obs_local):
+            v = jnp.exp(obs_all[s, o].astype(jnp.int32).astype(jnp.float32) * (1.0 / CODE_SCALE))
             for h in range(halves):
-                v = obs_all[s, o, :, h * LANES : (h + 1) * LANES]
-                totals[h] = totals[h] + v
-                first = (s * obs_local + o) * actions
-                obs_rows[first : first + actions, h, :] = v
+                part_h = v[:, h * LANES : (h + 1) * LANES]
+                totals[h] = totals[h] + part_h
+                obs_rows[s * actions : (s + 1) * actions, o * halves + h, :] = part_h
     for h in range(halves):
         tot_own[h] = totals[h]
     tot_cp = [
@@ -232,11 +263,27 @@
     for cp in tot_cp:
         cp.start()
 
+    share_cp = []
     for t in range(ny - 1):
         al_cp[t].wait_recv()
-        spread_alpha(lax.rem(y + ny - 1 - t, ny))
-
-    to_scalar.wait()
+        block = lax.rem(y + ny - 1 - t, ny)
+        cp = pltpu.make_async_remote_copy(
+            al_bf.at[block, c_rows],
+            al_bf.at[block, c_rows],
+            al2_send.at[t],
+            al2_recv.at[t],
+            device_id={"obs_2": 1 - c},
+            device_id_type=MESH,
+        )
+        cp.start()
+        share_cp.append(cp)
+        spread_alpha(block, c * half_y, half_y)
+    for t in range(ny - 1):
+        share_cp[t].wait_recv()
+        spread_alpha(lax.rem(y + ny - 1 - t, ny), (1 - c) * half_y, half_y)
+    for pair in to_scalar:
+        for cp in pair:
+            cp.wait()
     rs_cp = []
     for t in range(ng):
         j = g_at(t)
@@ -245,21 +292,17 @@
             b = j * own_rows + r
             a = act_s[b]
             sums = [None] * 4
-            n = 0
-            for s in range(nz):
+            for n in range(nz):
+                probs = obs_rows[n * actions + a]
                 for o in range(obs_local):
-                    k = pk_s[s * pk_len + o * pk_pitch + b]
-                    rows = al_rows[k]
-                    probs = obs_rows[(s * obs_local + o) * actions + a]
-                    term = rows * probs
-                    sums[n % 4] = term if sums[n % 4] is None else sums[n % 4] + term
-                    n += 1
+                    term = al_rows[pk_s[n][o][0, b]] * probs[o * halves : (o + 1) * halves]
+                    sums[o % 4] = term if n == 0 else sums[o % 4] + term
             part[pl.ds(pl.multiple_of(b * halves, halves), halves), :] = (sums[0] + sums[1]) + (
                 sums[2] + sums[3]
             )
             return carry
 
-        lax.fori_loop(0, own_rows, one_belief, 0)
+        lax.fori_loop(0, own_rows, one_belief, 0, unroll=2)
         if t < ng - 1:
             rows = own_rows * halves
             cp = pltpu.make_async_remote_copy(
@@ -396,7 +439,7 @@
     out_ref[:, q_cols] = fin[g]
     for cp in o_cp:
         cp.wait_recv()
-    for cp in ob_cp + pk_cp + al_cp + t_cp + tot_cp + rs_cp + w_cp + f_cp + tt_cp + o_cp:
+    for cp in ob_cp + pk_cp + al_cp + share_cp + t_cp + tot_cp + rs_cp + w_cp + f_cp + tt_cp + o_cp:
         cp.wait_send()
 
 
@@ -410,12 +453,6 @@
     qwidth = states // ng
     halves = width // LANES
     count = alpha_set.shape[0] * ny
-    hot = chosen_action[:, None] == jnp.arange(actions, dtype=jnp.int32)[None, :]
-    picks = jnp.sum(jnp.where(hot[:, :, None], chosen_idx, 0), axis=1).T
-    pitch = -(-bel // 256) * 256
-    picks = jnp.pad(picks, ((0, 0), (0, pitch - bel))).reshape(-1)
-    act_i = jnp.broadcast_to(chosen_action[:, None], (bel, LANES))
-    act_b = act_i.astype(jnp.bfloat16)
     f32, b16, i32 = jnp.float32, jnp.bfloat16, jnp.int32
     dma = pltpu.SemaphoreType.DMA
     vmem = pl.BlockSpec(memory_space=pltpu.VMEM)
@@ -425,10 +462,15 @@
     scratch = [
         pltpu.VMEM((ny, count // ny, width), b16),
         pltpu.VMEM((count, halves, LANES), f32),
-        pltpu.VMEM((nz, obs_local, actions, width), f32),
-        pltpu.VMEM((nz * obs_local * actions, halves, LANES), f32),
-        pltpu.VMEM((nz * obs_local * pitch,), i32),
-        pltpu.SMEM((nz * obs_local * pitch,), i32),
+        pltpu.VMEM((bel, LANES), i32),
+        pltpu.VMEM((bel, LANES), b16),
+        pltpu.VMEM((obs_local, actions, states), f32),
+        pltpu.VMEM((nz, obs_local, actions, width), jnp.int16),
+        pltpu.VMEM((nz, obs_local, actions, width), jnp.int16),
+        pltpu.VMEM((nz * actions, obs_local * halves, LANES), f32),
+        pltpu.VMEM((obs_local, 1, bel), i32),
+        pltpu.VMEM((nz, obs_local, 1, bel), i32),
+        [[pltpu.SMEM((1, bel), i32) for _ in range(obs_local)] for _ in range(nz)],
         pltpu.VMEM((bel * halves, LANES), f32),
         pltpu.VMEM((ng - 1, own_rows * halves, LANES), f32),
         pltpu.VMEM((halves, actions, LANES), f32),
@@ -442,9 +484,11 @@
         pltpu.VMEM((nz - 1, actions, qwidth), f32),
         pltpu.VMEM((actions, qwidth), f32),
         pltpu.VMEM((ng, bel // (nz * ng), qwidth), f32),
-        dma((6,)),
-        dma((nz - 1,)),
-        dma((nz - 1,)),
+        dma((5 + nz * obs_local,)),
+        dma((nz - 1,)),
+        dma((nz - 1,)),
+        dma((ny - 1,)),
+        dma((ny - 1,)),
         dma((ny - 1,)),
         dma((ny - 1,)),
         dma((nz - 1,)),
@@ -469,7 +513,6 @@
         out_shape=jax.ShapeDtypeStruct((bel // (nz * ng), states), f32),
         in_specs=[
             pl.BlockSpec(memory_space=pltpu.SMEM),
-            hbm,
             vmem,
             vmem,
             hbm,
@@ -483,7 +526,15 @@
             collective_id=0, has_side_effects=True, vmem_limit_bytes=60 * 1024 * 1024
         ),
         name="backup",
-    )(chosen_action, picks, act_i, act_b, alpha_set, transitions, obs_weights, rewards)
+    )(
+        chosen_action,
+        chosen_action.reshape(1, bel),
+        jnp.transpose(chosen_idx, (1, 2, 0)),
+        alpha_set,
+        transitions,
+        obs_weights,
+        rewards,
+    )
 
 
 def solution(mesh):

time: 86.3 us -> 75.3 us (0.87)
  Pallas kernels: 79.4 us -> 72.4 us
  other arithmetic: 2.31 us -> 0 us
  local copies, waits for them, and re-layouts: 4.3 us -> 2.72 us
    pallas_call x1, Pallas kernels: 79.4 us -> 72.4 us  [body(): pl.pallas_call(functools.partial(kernel, dims), out_shape=jax.ShapeDtypeS...]
    broadcast_in_dim x2 -> x0, local copies, waits for them, and re-layouts: 2.22 us -> none  [body(): act_i = jnp.broadcast_to(chosen_action[:, None], (bel, LANES))]
    reshape x0 -> x1, local copies, waits for them, and re-layouts: none -> 1.24 us  [body(): chosen_action.reshape(1, bel)]
    reduce_sum x1 -> x0, other arithmetic: 0.94 us -> none  [body(): picks = jnp.sum(jnp.where(hot[:, :, None], chosen_idx, 0), axis=1).T]
    unnamed x3 -> x1, local copies, waits for them, and re-layouts: 2.08 us -> 1.47 us
where the time goes in v2:
time: 75.3 us; the launch traced here: 75.1 us
  Pallas kernels  72.4 us (96%)
  local copies, waits for them, and re-layouts  2.72 us (4%)
    pallas_call x1, Pallas kernels, body(): pl.pallas_call(functools.partial(kernel, dims), out_shape=jax.ShapeDtypeS...  72.4 us

profile of v2, /device:TPU:1, one launch (start us, length us, event | category | flops | bytes accessed | tf_op | source)
XLA Modules:
  0.0 75.1 jit_solution(10986705030862965086)
XLA Ops:
  0.0 1.2 %reshape.3.act_row = s32[1,384]{1,0:T(1,128)} reshape(s32[384]{0:T(512)} %act_s.1) | data formatting | bytes 3072 | tf_op jit(solution)/shard_map/reshape | solution.py:531
  1.2 72.4 %backup.1 = f32[6,2048]{1,0:T(8,128)} custom-call(s32[384]{0:T(512)} %act_s.1, s32[1,384]{1,0:T(1,128)} %reshape.3.act_row, s32[16,4,384]{2,1,0:T(4,128)} %bitcast.1, bf16[512,2048]{1,0:T(8,128)(2,1)} %alpha_hbm.1, bf16[16,32,2048]{2,1,0:T(8,128)(2,1)} %trans_hbm.1, f32[4,16,2048]{2,1,0:T(8,128)} %obs_hbm.1, f32[16,2048]{1,0:T(8,128)} %rew_hbm.1), custom_call_target="tpu_custom_call" | custom-call | tf_op jit(solution)/shard_map/backup/pallas_call | solution.py:511
  73.6 1.5 %copy.8 = f32[6,2048]{1,0:T(8,128)} copy(f32[6,2048]{1,0:T(8,128)} %backup.1) | data formatting | bytes 98304

commit v3 on v2

--- a/solution.py
+++ b/solution.py
@@ -15,6 +15,23 @@
 CODE_SCALE = 14114.0
 CODE_SHIFT = 2.302585093 * CODE_SCALE
 MESH = pl.DeviceIdType.MESH
+
+
+def to_codes(values):
+    largest = functools.reduce(
+        jnp.maximum, [jnp.max(jnp.abs(v), axis=(0, 1), keepdims=True) for v in values]
+    )
+    level = jnp.ceil(32.0 * jnp.log(jnp.maximum(largest, 1e-30) * (1.0 / 32760.0)))
+    inverse = jnp.exp(level * (-1.0 / 32.0))
+    coded = [
+        jnp.clip(jnp.round(v * inverse), -32767.0, 32767.0).astype(jnp.int32).astype(jnp.int16)
+        for v in values
+    ]
+    return coded, jnp.broadcast_to(level, (8, LANES)).astype(jnp.int32).astype(jnp.int16)
+
+
+def scale_of(level):
+    return jnp.exp(level.astype(jnp.int32).astype(jnp.float32) * (1.0 / 32.0))
 
 
 def kernel(
@@ -45,7 +62,9 @@
     w_all,
     t_blk,
     spread,
+    w_scale,
     fut,
+    fut_q,
     f_buf,
     tt_own,
     tt_buf,
@@ -62,6 +81,10 @@
     ob_recv,
     t_send,
     t_recv,
+    ts_send,
+    ts_recv,
+    ty_send,
+    ty_recv,
     tot_send,
     tot_recv,
     rs_send,
@@ -89,6 +112,8 @@
     obs_local = obs_hbm.shape[0]
     t_rows = trans_hbm.shape[1]
     last = fin.shape[1]
+    per_y = actions // (2 * ny)
+    direct = actions - per_y * ny
 
     y = lax.axis_index("bel")
     z = lax.axis_index("obs_0")
@@ -129,15 +154,19 @@
 
     own_al = pltpu.make_async_copy(alpha_hbm.at[:, z_cols], al_bf.at[y], local_sem.at[1])
     own_ob = pltpu.make_async_copy(obs_hbm, obs_v, local_sem.at[2])
+    g_rows = pl.ds(pl.multiple_of(g * t_rows, t_rows), t_rows)
+    mine = pl.ds(direct + y * per_y, per_y)
     own_t = pltpu.make_async_copy(
-        trans_hbm.at[:, :, q_cols],
-        t_blk.at[:, pl.ds(pl.multiple_of(g * t_rows, t_rows), t_rows), :],
-        local_sem.at[3],
+        trans_hbm.at[:direct, :, q_cols], t_blk.at[:direct, g_rows, :], local_sem.at[3]
+    )
+    own_ts = pltpu.make_async_copy(
+        trans_hbm.at[mine, :, q_cols], t_blk.at[mine, g_rows, :], local_sem.at[0]
     )
     own_rew = pltpu.make_async_copy(rew_hbm.at[:, q_cols], rew_v, local_sem.at[4])
     own_ob.start()
     own_al.start()
     own_t.start()
+    own_ts.start()
     own_rew.start()
 
     picks = jnp.zeros((obs_local, bel), jnp.int32)
@@ -194,22 +223,25 @@
         )
         for t in range(nz - 1)
     ]
-    t_cp = [
-        pltpu.make_async_remote_copy(
-            trans_hbm.at[:, :, pl.ds(pl.multiple_of(g_at(t) * qwidth, qwidth), qwidth)],
-            t_blk.at[:, pl.ds(pl.multiple_of(g * t_rows, t_rows), t_rows), :],
-            t_send.at[t],
-            t_recv.at[t],
+    def trans_copy(t, which, send, recv):
+        return pltpu.make_async_remote_copy(
+            trans_hbm.at[which, :, pl.ds(pl.multiple_of(g_at(t) * qwidth, qwidth), qwidth)],
+            t_blk.at[which, g_rows, :],
+            send.at[t],
+            recv.at[t],
             device_id=to_g(t),
             device_id_type=MESH,
         )
-        for t in range(ng - 1)
-    ]
+
+    ts_cp = [trans_copy(t, mine, ts_send, ts_recv) for t in range(ng - 1)]
+    t_cp = [trans_copy(t, pl.ds(0, direct), t_send, t_recv) for t in range(ng - 1)]
     for cp in pk_cp:
         cp.start()
     for cp in al_cp:
         cp.start()
     for cp in ob_cp:
+        cp.start()
+    for cp in ts_cp:
         cp.start()
     for cp in t_cp:
         cp.start()
@@ -281,6 +313,22 @@
     for t in range(ny - 1):
         share_cp[t].wait_recv()
         spread_alpha(lax.rem(y + ny - 1 - t, ny), (1 - c) * half_y, half_y)
+    own_ts.wait()
+    for cp in ts_cp:
+        cp.wait_recv()
+    ty_cp = [
+        pltpu.make_async_remote_copy(
+            t_blk.at[mine],
+            t_blk.at[mine],
+            ty_send.at[t],
+            ty_recv.at[t],
+            device_id=to_y(t),
+            device_id_type=MESH,
+        )
+        for t in range(ny - 1)
+    ]
+    for cp in ty_cp:
+        cp.start()
     for pair in to_scalar:
         for cp in pair:
             cp.wait()
@@ -321,6 +369,7 @@
     for cp in rs_cp:
         cp.wait_recv()
     act_own = act_i[pl.ds(pl.multiple_of(g * own_rows, own_rows), own_rows), :]
+    values = []
     for h in range(halves):
         total = tot_own[h]
         for t in range(ng - 1):
@@ -331,11 +380,12 @@
         divisor = jnp.ones((own_rows, LANES), jnp.float32)
         for a in range(actions):
             divisor = jnp.where(act_own == a, total[a : a + 1, :], divisor)
-        w = raw / divisor
-        hi = w.astype(jnp.bfloat16)
-        lo = (w - hi.astype(jnp.float32)).astype(jnp.bfloat16)
-        w_all[g, 0, :, h * LANES : (h + 1) * LANES] = hi
-        w_all[g, 1, :, h * LANES : (h + 1) * LANES] = lo
+        values.append(raw / divisor)
+    coded, level = to_codes(values)
+    for h in range(halves):
+        cols = slice(h * LANES, (h + 1) * LANES)
+        w_all[g, :own_rows, cols] = coded[h]
+        w_all[g, own_rows:, cols] = level
 
     w_cp = [
         pltpu.make_async_remote_copy(
@@ -345,34 +395,64 @@
     ]
     for cp in w_cp:
         cp.start()
-    for cp in w_cp:
-        cp.wait_recv()
-
-    def spread_action(a, carry):
-        hot = act_b[...] == a.astype(jnp.bfloat16)
-        for k in range(2):
+
+    def spread_owner(j):
+        rows = pl.ds(pl.multiple_of(j * own_rows, own_rows), own_rows)
+        low_rows = pl.ds(pl.multiple_of(bel + j * own_rows, own_rows), own_rows)
+        w_scale[rows, :] = jnp.broadcast_to(
+            scale_of(w_all[j, own_rows : own_rows + 1, :]), (own_rows, width)
+        )[:, :qwidth]
+        act = act_b[rows, :]
+        pieces = []
+        for h in range(halves):
+            q = w_all[j, :own_rows, h * LANES : (h + 1) * LANES].astype(jnp.int32)
+            high = jnp.right_shift(q + 128, 8)
+            low = q - jnp.left_shift(high, 8)
+            pieces.append((high.astype(jnp.float32).astype(jnp.bfloat16), low.astype(jnp.float32).astype(jnp.bfloat16)))
+
+        for a in range(actions):
+            hot = act == jnp.asarray(a, jnp.bfloat16)
             for h in range(halves):
-                val = w_all[:, k, :, h * LANES : (h + 1) * LANES].reshape(bel, LANES)
-                spread[
-                    k * bel : (k + 1) * bel,
-                    pl.ds(pl.multiple_of(a * width + h * LANES, LANES), LANES),
-                ] = jnp.where(hot, val, jnp.zeros_like(val))
-        return carry
-
-    lax.fori_loop(0, actions, spread_action, 0)
-
+                high, low = pieces[h]
+                cols = slice(a * width + h * LANES, a * width + (h + 1) * LANES)
+                spread[rows, cols] = jnp.where(hot, high, jnp.zeros_like(high))
+                spread[low_rows, cols] = jnp.where(hot, low, jnp.zeros_like(low))
+
+    spread_owner(g)
     own_t.wait()
     for cp in t_cp:
         cp.wait_recv()
+    for cp in ty_cp:
+        cp.wait_recv()
+
+    def total_action(a, carry):
+        tt_own[pl.ds(a, 1), :] = jnp.sum(
+            t_blk[a].astype(jnp.float32), axis=0, keepdims=True
+        )
+        return carry
+
+    lax.fori_loop(0, actions, total_action, 0)
+    tt_cp = [
+        pltpu.make_async_remote_copy(
+            tt_own, tt_buf.at[t], tt_send.at[t], tt_recv.at[t], device_id=to_z(t), device_id_type=MESH
+        )
+        for t in range(nz - 1)
+    ]
+    for cp in tt_cp:
+        cp.start()
+
+    for t in range(ng - 1):
+        w_cp[t].wait_recv()
+        spread_owner(lax.rem(g + ng - 1 - t, ng))
     both = jnp.dot(
         spread[...],
         t_blk[...].reshape(actions * width, qwidth),
         preferred_element_type=jnp.float32,
     )
-    fut[...] = both[:bel] + both[bel:]
+    fut[...] = (256.0 * both[:bel] + both[bel:]) * w_scale[...]
     f_cp = [
         pltpu.make_async_remote_copy(
-            fut.at[pl.ds(pl.multiple_of(z_at(t) * z_rows, z_rows), z_rows), :],
+            fut_q.at[z_at(t)],
             f_buf.at[t],
             f_send.at[t],
             f_recv.at[t],
@@ -381,24 +461,14 @@
         )
         for t in range(nz - 1)
     ]
-    for cp in f_cp:
-        cp.start()
-
-    def total_action(a, carry):
-        tt_own[pl.ds(a, 1), :] = jnp.sum(
-            t_blk[a].astype(jnp.float32), axis=0, keepdims=True
-        )
-        return carry
-
-    lax.fori_loop(0, actions, total_action, 0)
-    tt_cp = [
-        pltpu.make_async_remote_copy(
-            tt_own, tt_buf.at[t], tt_send.at[t], tt_recv.at[t], device_id=to_z(t), device_id_type=MESH
-        )
-        for t in range(nz - 1)
-    ]
-    for cp in tt_cp:
-        cp.start()
+    for t in range(nz - 1):
+        j = z_at(t)
+        rows = pl.ds(pl.multiple_of(j * z_rows, z_rows), z_rows)
+        (coded,), level = to_codes([fut[rows, :]])
+        fut_q[j, :z_rows, :] = coded
+        for h in range(qwidth // LANES):
+            fut_q[j, z_rows:, h * LANES : (h + 1) * LANES] = level
+        f_cp[t].start()
     own_rew.wait()
     for cp in f_cp:
         cp.wait_recv()
@@ -413,7 +483,8 @@
             total = total + tt_buf[t, :, cols]
         future = fut[pl.ds(z_start, z_rows), cols]
         for t in range(nz - 1):
-            future = future + f_buf[t, :, cols]
+            piece = f_buf[t, :z_rows, cols].astype(jnp.int32).astype(jnp.float32)
+            future = future + piece * scale_of(f_buf[t, z_rows : z_rows + 1, cols])
         divisor = jnp.ones((z_rows, LANES), jnp.float32)
         reward = jnp.zeros((z_rows, LANES), jnp.float32)
         for a in range(actions):
@@ -439,7 +510,7 @@
     out_ref[:, q_cols] = fin[g]
     for cp in o_cp:
         cp.wait_recv()
-    for cp in ob_cp + pk_cp + al_cp + share_cp + t_cp + tot_cp + rs_cp + w_cp + f_cp + tt_cp + o_cp:
+    for cp in ob_cp + pk_cp + al_cp + share_cp + ts_cp + ty_cp + t_cp + tot_cp + rs_cp + w_cp + f_cp + tt_cp + o_cp:
         cp.wait_send()
 
 
@@ -475,11 +546,13 @@
         pltpu.VMEM((ng - 1, own_rows * halves, LANES), f32),
         pltpu.VMEM((halves, actions, LANES), f32),
         pltpu.VMEM((ng - 1, halves, actions, LANES), f32),
-        pltpu.VMEM((ng, 2, own_rows, width), b16),
+        pltpu.VMEM((ng, own_rows + 8, width), jnp.int16),
         pltpu.VMEM((actions, width, qwidth), b16),
         pltpu.VMEM((2 * bel, actions * width), b16),
         pltpu.VMEM((bel, qwidth), f32),
-        pltpu.VMEM((nz - 1, z_rows, qwidth), f32),
+        pltpu.VMEM((bel, qwidth), f32),
+        pltpu.VMEM((nz, z_rows + 8, qwidth), jnp.int16),
+        pltpu.VMEM((nz - 1, z_rows + 8, qwidth), jnp.int16),
         pltpu.VMEM((actions, qwidth), f32),
         pltpu.VMEM((nz - 1, actions, qwidth), f32),
         pltpu.VMEM((actions, qwidth), f32),
@@ -495,6 +568,10 @@
         dma((nz - 1,)),
         dma((ng - 1,)),
         dma((ng - 1,)),
+        dma((ng - 1,)),
+        dma((ng - 1,)),
+        dma((ny - 1,)),
+        dma((ny - 1,)),
         dma((ng - 1,)),
         dma((ng - 1,)),
         dma((ng - 1,)),

time: 75.3 us -> 59.8 us (0.79)
  Pallas kernels: 72.4 us -> 56.9 us
    pallas_call x1, Pallas kernels: 72.4 us -> 56.9 us  [body(): pl.pallas_call(functools.partial(kernel, dims), out_shape=jax.ShapeDtypeS...]
where the time goes in v3:
time: 59.8 us; the launch traced here: 59.7 us
  Pallas kernels  56.9 us (95%)
  local copies, waits for them, and re-layouts  2.72 us (5%)
    pallas_call x1, Pallas kernels, body(): pl.pallas_call(functools.partial(kernel, dims), out_shape=jax.ShapeDtypeS...  56.9 us
    unnamed x1, local copies, waits for them, and re-layouts  1.47 us
    reshape x1, local copies, waits for them, and re-layouts, body(): chosen_action.reshape(1, bel)  1.24 us

profile of v3, /device:TPU:1, one launch (start us, length us, event | category | flops | bytes accessed | tf_op | source)
XLA Modules:
  0.0 59.7 jit_solution(15744022191292817828)
XLA Ops:
  0.0 1.2 %reshape.3.act_row = s32[1,384]{1,0:T(1,128)} reshape(s32[384]{0:T(512)} %act_s.1) | data formatting | bytes 3072 | tf_op jit(solution)/shard_map/reshape | solution.py:608
  1.2 56.9 %backup.1 = f32[6,2048]{1,0:T(8,128)} custom-call(s32[384]{0:T(512)} %act_s.1, s32[1,384]{1,0:T(1,128)} %reshape.3.act_row, s32[16,4,384]{2,1,0:T(4,128)} %bitcast.1, bf16[512,2048]{1,0:T(8,128)(2,1)} %alpha_hbm.1, bf16[16,32,2048]{2,1,0:T(8,128)(2,1)} %trans_hbm.1, f32[4,16,2048]{2,1,0:T(8,128)} %obs_hbm.1, f32[16,2048]{1,0:T(8,128)} %rew_hbm.1), custom_call_target="tpu_custom_call" | custom-call | tf_op jit(solution)/shard_map/backup/pallas_call | solution.py:588
  58.2 1.5 %copy.8 = f32[6,2048]{1,0:T(8,128)} copy(f32[6,2048]{1,0:T(8,128)} %backup.1) | data formatting | bytes 98304

commit v4 on v3

--- a/solution.py
+++ b/solution.py
@@ -32,6 +32,10 @@
 
 def scale_of(level):
     return jnp.exp(level.astype(jnp.int32).astype(jnp.float32) * (1.0 / 32.0))
+
+
+def far_first(n):
+    return sorted(range(n - 1), key=lambda t: -min(t + 1, n - 1 - t))
 
 
 def kernel(
@@ -75,8 +79,10 @@
     pk_recv,
     al_send,
     al_recv,
-    al2_send,
-    al2_recv,
+    relay_send,
+    relay_recv,
+    share_send,
+    share_recv,
     ob_send,
     ob_recv,
     t_send,
@@ -171,7 +177,7 @@
 
     picks = jnp.zeros((obs_local, bel), jnp.int32)
     for a in range(actions):
-        picks = jnp.where(act_row[...] == a, idx_ref[a], picks)
+        picks = jnp.where(act_row[...] == a, idx_ref[a] * halves, picks)
     for o in range(obs_local):
         pk_own[o] = picks[o : o + 1, :]
         pk_v[z, o] = picks[o : o + 1, :]
@@ -207,10 +213,10 @@
             al_bf.at[y, c_rows],
             al_send.at[t],
             al_recv.at[t],
-            device_id=to_y(t),
-            device_id_type=MESH,
-        )
-        for t in range(ny - 1)
+            device_id={"bel": lax.rem(y + step, ny)},
+            device_id_type=MESH,
+        )
+        for t, step in ((0, 1), (1, ny - 1))
     ]
     ob_cp = [
         pltpu.make_async_remote_copy(
@@ -239,8 +245,8 @@
         cp.start()
     for cp in al_cp:
         cp.start()
-    for cp in ob_cp:
-        cp.start()
+    for t in far_first(nz):
+        ob_cp[t].start()
     for cp in ts_cp:
         cp.start()
     for cp in t_cp:
@@ -251,7 +257,9 @@
             r = pl.multiple_of(start + n * 16, 16)
             v = al_bf[block, pl.ds(r, 16), :].astype(jnp.float32)
             for h in range(halves):
-                al_rows[pl.ds(block * rows_y + r, 16), h, :] = v[:, h * LANES : (h + 1) * LANES]
+                al_rows[pl.ds((block * rows_y + r) * halves + h, 16, stride=halves), :] = v[
+                    :, h * LANES : (h + 1) * LANES
+                ]
             return carry
 
         lax.fori_loop(0, rows // 16, rows16, 0, unroll=4)
@@ -272,18 +280,59 @@
         for cp in pair:
             cp.start()
 
-    for o in range(obs_local):
-        obs_all[z, o] = obs_code[z, o]
-    for cp in ob_cp:
-        cp.wait_recv()
     totals = [jnp.zeros((actions, LANES), jnp.float32) for _ in range(halves)]
-    for s in range(nz):
+
+    def decode(code_ref, slot):
         for o in range(obs_local):
-            v = jnp.exp(obs_all[s, o].astype(jnp.int32).astype(jnp.float32) * (1.0 / CODE_SCALE))
+            v = jnp.exp(
+                code_ref[slot, o].astype(jnp.int32).astype(jnp.float32) * (1.0 / CODE_SCALE)
+            )
             for h in range(halves):
                 part_h = v[:, h * LANES : (h + 1) * LANES]
                 totals[h] = totals[h] + part_h
-                obs_rows[s * actions : (s + 1) * actions, o * halves + h, :] = part_h
+                obs_rows[pl.ds(slot * actions, actions), o * halves + h, :] = part_h
+
+    decode(obs_code, z)
+    share_cp = []
+
+    def share(block, rows):
+        cp = pltpu.make_async_remote_copy(
+            al_bf.at[block, rows],
+            al_bf.at[block, rows],
+            share_send.at[len(share_cp)],
+            share_recv.at[len(share_cp)],
+            device_id={"obs_2": 1 - c},
+            device_id_type=MESH,
+        )
+        cp.start()
+        share_cp.append(cp)
+
+    before, after, across = (lax.rem(y + n, ny) for n in (ny - 1, 1, ny - 2))
+    quarter = half_y // 2
+    quarters = [pl.ds(pl.multiple_of(c * half_y + n * quarter, quarter), quarter) for n in range(2)]
+    relay_cp = []
+    for t, (source, target) in enumerate(((before, after), (after, before))):
+        al_cp[t].wait_recv()
+        cp = pltpu.make_async_remote_copy(
+            al_bf.at[source, quarters[t]],
+            al_bf.at[source, quarters[t]],
+            relay_send.at[t],
+            relay_recv.at[t],
+            device_id={"bel": target},
+            device_id_type=MESH,
+        )
+        cp.start()
+        relay_cp.append(cp)
+        share(source, c_rows)
+    for source in (before, after):
+        spread_alpha(source, c * half_y, half_y)
+    for t in range(2):
+        relay_cp[t].wait_recv()
+        share(across, quarters[t])
+    spread_alpha(across, c * half_y, half_y)
+    for t in far_first(nz):
+        ob_cp[t].wait_recv()
+        decode(obs_all, lax.rem(z + nz - 1 - t, nz))
     for h in range(halves):
         tot_own[h] = totals[h]
     tot_cp = [
@@ -295,24 +344,18 @@
     for cp in tot_cp:
         cp.start()
 
-    share_cp = []
-    for t in range(ny - 1):
-        al_cp[t].wait_recv()
-        block = lax.rem(y + ny - 1 - t, ny)
-        cp = pltpu.make_async_remote_copy(
-            al_bf.at[block, c_rows],
-            al_bf.at[block, c_rows],
-            al2_send.at[t],
-            al2_recv.at[t],
-            device_id={"obs_2": 1 - c},
-            device_id_type=MESH,
-        )
-        cp.start()
-        share_cp.append(cp)
-        spread_alpha(block, c * half_y, half_y)
-    for t in range(ny - 1):
-        share_cp[t].wait_recv()
-        spread_alpha(lax.rem(y + ny - 1 - t, ny), (1 - c) * half_y, half_y)
+    other = (1 - c) * half_y
+    for cp, (source, start, rows) in zip(
+        share_cp,
+        (
+            (before, other, half_y),
+            (after, other, half_y),
+            (across, other, quarter),
+            (across, other + quarter, quarter),
+        ),
+    ):
+        cp.wait_recv()
+        spread_alpha(source, start, rows)
     own_ts.wait()
     for cp in ts_cp:
         cp.wait_recv()
@@ -343,14 +386,14 @@
             for n in range(nz):
                 probs = obs_rows[n * actions + a]
                 for o in range(obs_local):
-                    term = al_rows[pk_s[n][o][0, b]] * probs[o * halves : (o + 1) * halves]
+                    term = al_rows[pl.ds(pk_s[n][o][0, b], halves), :] * probs[o * halves : (o + 1) * halves]
                     sums[o % 4] = term if n == 0 else sums[o % 4] + term
             part[pl.ds(pl.multiple_of(b * halves, halves), halves), :] = (sums[0] + sums[1]) + (
                 sums[2] + sums[3]
             )
             return carry
 
-        lax.fori_loop(0, own_rows, one_belief, 0, unroll=2)
+        lax.fori_loop(0, own_rows, one_belief, 0, unroll=4)
         if t < ng - 1:
             rows = own_rows * halves
             cp = pltpu.make_async_remote_copy(
@@ -398,7 +441,11 @@
 
     def spread_owner(j):
         rows = pl.ds(pl.multiple_of(j * own_rows, own_rows), own_rows)
-        low_rows = pl.ds(pl.multiple_of(bel + j * own_rows, own_rows), own_rows)
+        half = j // (ng // 2)
+        high_rows = pl.ds(pl.multiple_of((half * (ng // 2) + j) * own_rows, own_rows), own_rows)
+        low_rows = pl.ds(
+            pl.multiple_of((half * (ng // 2) + j) * own_rows + bel // 2, own_rows), own_rows
+        )
         w_scale[rows, :] = jnp.broadcast_to(
             scale_of(w_all[j, own_rows : own_rows + 1, :]), (own_rows, width)
         )[:, :qwidth]
@@ -415,7 +462,7 @@
             for h in range(halves):
                 high, low = pieces[h]
                 cols = slice(a * width + h * LANES, a * width + (h + 1) * LANES)
-                spread[rows, cols] = jnp.where(hot, high, jnp.zeros_like(high))
+                spread[high_rows, cols] = jnp.where(hot, high, jnp.zeros_like(high))
                 spread[low_rows, cols] = jnp.where(hot, low, jnp.zeros_like(low))
 
     spread_owner(g)
@@ -444,31 +491,44 @@
     for t in range(ng - 1):
         w_cp[t].wait_recv()
         spread_owner(lax.rem(g + ng - 1 - t, ng))
-    both = jnp.dot(
-        spread[...],
-        t_blk[...].reshape(actions * width, qwidth),
-        preferred_element_type=jnp.float32,
-    )
-    fut[...] = (256.0 * both[:bel] + both[bel:]) * w_scale[...]
-    f_cp = [
-        pltpu.make_async_remote_copy(
-            fut_q.at[z_at(t)],
-            f_buf.at[t],
-            f_send.at[t],
-            f_recv.at[t],
-            device_id=to_z(t),
-            device_id_type=MESH,
-        )
-        for t in range(nz - 1)
-    ]
-    for t in range(nz - 1):
-        j = z_at(t)
+    half_bel = bel // 2
+    group = nz // 2
+
+    def future_half(half):
+        rows = pl.ds(pl.multiple_of(half * half_bel, half_bel), half_bel)
+        both = jnp.dot(
+            spread[pl.ds(pl.multiple_of(half * bel, bel), bel), :],
+            t_blk[...].reshape(actions * width, qwidth),
+            preferred_element_type=jnp.float32,
+        )
+        fut[rows, :] = (256.0 * both[:half_bel] + both[half_bel:]) * w_scale[rows, :]
+
+    def send_future(j, t):
         rows = pl.ds(pl.multiple_of(j * z_rows, z_rows), z_rows)
         (coded,), level = to_codes([fut[rows, :]])
         fut_q[j, :z_rows, :] = coded
         for h in range(qwidth // LANES):
             fut_q[j, z_rows:, h * LANES : (h + 1) * LANES] = level
-        f_cp[t].start()
+        cp = pltpu.make_async_remote_copy(
+            fut_q.at[j],
+            f_buf.at[t],
+            f_send.at[t],
+            f_recv.at[t],
+            device_id={"obs_0": j},
+            device_id_type=MESH,
+        )
+        cp.start()
+        f_cp.append(cp)
+
+    f_cp = []
+    z_half = z // group
+    far_half = 1 - z_half
+    future_half(far_half)
+    for n in range(group):
+        send_future(far_half * group + lax.rem(z + n, group), n)
+    future_half(z_half)
+    for n in range(1, group):
+        send_future(z_half * group + lax.rem(z + n, group), group - 1 + n)
     own_rew.wait()
     for cp in f_cp:
         cp.wait_recv()
@@ -510,7 +570,7 @@
     out_ref[:, q_cols] = fin[g]
     for cp in o_cp:
         cp.wait_recv()
-    for cp in ob_cp + pk_cp + al_cp + share_cp + ts_cp + ty_cp + t_cp + tot_cp + rs_cp + w_cp + f_cp + tt_cp + o_cp:
+    for cp in ob_cp + pk_cp + al_cp + share_cp + ts_cp + ty_cp + t_cp + relay_cp + tot_cp + rs_cp + w_cp + f_cp + tt_cp + o_cp:
         cp.wait_send()
 
 
@@ -532,7 +592,7 @@
     own_rows = bel // ng
     scratch = [
         pltpu.VMEM((ny, count // ny, width), b16),
-        pltpu.VMEM((count, halves, LANES), f32),
+        pltpu.VMEM((count * halves, LANES), f32),
         pltpu.VMEM((bel, LANES), i32),
         pltpu.VMEM((bel, LANES), b16),
         pltpu.VMEM((obs_local, actions, states), f32),
@@ -560,10 +620,12 @@
         dma((5 + nz * obs_local,)),
         dma((nz - 1,)),
         dma((nz - 1,)),
-        dma((ny - 1,)),
-        dma((ny - 1,)),
-        dma((ny - 1,)),
-        dma((ny - 1,)),
+        dma((2,)),
+        dma((2,)),
+        dma((2,)),
+        dma((2,)),
+        dma((4,)),
+        dma((4,)),
         dma((nz - 1,)),
         dma((nz - 1,)),
         dma((ng - 1,)),

time: 59.8 us -> 57.2 us (0.957)
  Pallas kernels: 56.9 us -> 54.2 us
    pallas_call x1, Pallas kernels: 56.9 us -> 54.2 us  [body(): pl.pallas_call(functools.partial(kernel, dims), out_shape=jax.ShapeDtypeS...]
where the time goes in v4:
time: 57.2 us; the launch traced here: 57 us
  Pallas kernels  54.2 us (95%)
  local copies, waits for them, and re-layouts  2.72 us (5%)
    pallas_call x1, Pallas kernels, body(): pl.pallas_call(functools.partial(kernel, dims), out_shape=jax.ShapeDtypeS...  54.2 us
    unnamed x1, local copies, waits for them, and re-layouts  1.47 us
    reshape x1, local copies, waits for them, and re-layouts, body(): chosen_action.reshape(1, bel)  1.24 us

profile of v4, /device:TPU:1, one launch (start us, length us, event | category | flops | bytes accessed | tf_op | source)
XLA Modules:
  0.0 57.0 jit_solution(414249483409537943)
XLA Ops:
  0.0 1.2 %reshape.3.act_row = s32[1,384]{1,0:T(1,128)} reshape(s32[384]{0:T(512)} %act_s.1) | data formatting | bytes 3072 | tf_op jit(solution)/shard_map/reshape | solution.py:670
  1.2 54.2 %backup.1 = f32[6,2048]{1,0:T(8,128)} custom-call(s32[384]{0:T(512)} %act_s.1, s32[1,384]{1,0:T(1,128)} %reshape.3.act_row, s32[16,4,384]{2,1,0:T(4,128)} %bitcast.1, bf16[512,2048]{1,0:T(8,128)(2,1)} %alpha_hbm.1, bf16[16,32,2048]{2,1,0:T(8,128)(2,1)} %trans_hbm.1, f32[4,16,2048]{2,1,0:T(8,128)} %obs_hbm.1, f32[16,2048]{1,0:T(8,128)} %rew_hbm.1), custom_call_target="tpu_custom_call" | custom-call | tf_op jit(solution)/shard_map/backup/pallas_call | solution.py:650
  55.5 1.5 %copy.8 = f32[6,2048]{1,0:T(8,128)} copy(f32[6,2048]{1,0:T(8,128)} %backup.1) | data formatting | bytes 98304

commit v5 on v4

--- a/solution.py
+++ b/solution.py
@@ -36,6 +36,11 @@
 
 def far_first(n):
     return sorted(range(n - 1), key=lambda t: -min(t + 1, n - 1 - t))
+
+
+def group_offsets(nx, nc):
+    steps = [(dx, dc) for dx in range(nx) for dc in range(nc) if dx or dc]
+    return sorted(steps, key=lambda step: -min(step[0], nx - step[0]))
 
 
 def kernel(
@@ -133,8 +138,15 @@
     def z_at(t):
         return lax.rem(z + 1 + t, nz)
 
+    offsets = group_offsets(nx, nc)
+
     def g_at(t):
-        return lax.rem(g + 1 + t, ng)
+        dx, dc = offsets[t]
+        return lax.rem(x + dx, nx) * nc + lax.rem(c + dc, nc)
+
+    def g_from(t):
+        dx, dc = offsets[t]
+        return lax.rem(x + nx - dx, nx) * nc + lax.rem(c + nc - dc, nc)
 
     def to_y(t):
         return {"bel": y_at(t)}
@@ -195,7 +207,8 @@
             obs_code[n, o] = jnp.round(v * CODE_SCALE + CODE_SHIFT).astype(jnp.int32).astype(jnp.int16)
     pl.semaphore_wait(barrier, len(peers))
 
-    c_rows = pl.ds(pl.multiple_of(c * half_y, half_y), half_y)
+    quarter = half_y // 2
+    quarters = [pl.ds(pl.multiple_of(c * half_y + n * quarter, quarter), quarter) for n in range(2)]
     pk_cp = [
         pltpu.make_async_remote_copy(
             pk_own,
@@ -208,14 +221,17 @@
         for t in range(nz - 1)
     ]
     al_cp = [
-        pltpu.make_async_remote_copy(
-            alpha_hbm.at[c_rows, z_cols],
-            al_bf.at[y, c_rows],
-            al_send.at[t],
-            al_recv.at[t],
-            device_id={"bel": lax.rem(y + step, ny)},
-            device_id_type=MESH,
-        )
+        [
+            pltpu.make_async_remote_copy(
+                al_bf.at[y, quarters[n]],
+                al_bf.at[y, quarters[n]],
+                al_send.at[t, m],
+                al_recv.at[t, m],
+                device_id={"bel": lax.rem(y + step, ny)},
+                device_id_type=MESH,
+            )
+            for m, n in enumerate((t, 1 - t))
+        ]
         for t, step in ((0, 1), (1, ny - 1))
     ]
     ob_cp = [
@@ -243,8 +259,10 @@
     t_cp = [trans_copy(t, pl.ds(0, direct), t_send, t_recv) for t in range(ng - 1)]
     for cp in pk_cp:
         cp.start()
-    for cp in al_cp:
-        cp.start()
+    own_al.wait()
+    for m in range(2):
+        for pair in al_cp:
+            pair[m].start()
     for t in far_first(nz):
         ob_cp[t].start()
     for cp in ts_cp:
@@ -264,7 +282,6 @@
 
         lax.fori_loop(0, rows // 16, rows16, 0, unroll=4)
 
-    own_al.wait()
     spread_alpha(y, 0, rows_y)
 
     for cp in pk_cp:
@@ -308,11 +325,9 @@
         share_cp.append(cp)
 
     before, after, across = (lax.rem(y + n, ny) for n in (ny - 1, 1, ny - 2))
-    quarter = half_y // 2
-    quarters = [pl.ds(pl.multiple_of(c * half_y + n * quarter, quarter), quarter) for n in range(2)]
     relay_cp = []
     for t, (source, target) in enumerate(((before, after), (after, before))):
-        al_cp[t].wait_recv()
+        al_cp[t][0].wait_recv()
         cp = pltpu.make_async_remote_copy(
             al_bf.at[source, quarters[t]],
             al_bf.at[source, quarters[t]],
@@ -323,7 +338,28 @@
         )
         cp.start()
         relay_cp.append(cp)
-        share(source, c_rows)
+    for t, source in enumerate((before, after)):
+        share(source, quarters[t])
+    for t, source in enumerate((before, after)):
+        al_cp[t][1].wait_recv()
+        share(source, quarters[1 - t])
+    own_ts.wait()
+    for cp in ts_cp:
+        cp.wait_recv()
+
+    def trans_share(which, n, target):
+        return pltpu.make_async_remote_copy(
+            t_blk.at[which],
+            t_blk.at[which],
+            ty_send.at[n],
+            ty_recv.at[n],
+            device_id={"bel": target},
+            device_id_type=MESH,
+        )
+
+    ty_cp = [trans_share(mine, 0, after), trans_share(mine, 1, before)]
+    for cp in ty_cp:
+        cp.start()
     for source in (before, after):
         spread_alpha(source, c * half_y, half_y)
     for t in range(2):
@@ -345,39 +381,17 @@
         cp.start()
 
     other = (1 - c) * half_y
-    for cp, (source, start, rows) in zip(
-        share_cp,
-        (
-            (before, other, half_y),
-            (after, other, half_y),
-            (across, other, quarter),
-            (across, other + quarter, quarter),
-        ),
+    for cp, (source, n) in zip(
+        share_cp, ((before, 0), (after, 1), (before, 1), (after, 0), (across, 0), (across, 1))
     ):
         cp.wait_recv()
-        spread_alpha(source, start, rows)
-    own_ts.wait()
-    for cp in ts_cp:
-        cp.wait_recv()
-    ty_cp = [
-        pltpu.make_async_remote_copy(
-            t_blk.at[mine],
-            t_blk.at[mine],
-            ty_send.at[t],
-            ty_recv.at[t],
-            device_id=to_y(t),
-            device_id_type=MESH,
-        )
-        for t in range(ny - 1)
-    ]
-    for cp in ty_cp:
-        cp.start()
+        spread_alpha(source, other + n * quarter, quarter)
     for pair in to_scalar:
         for cp in pair:
             cp.wait()
     rs_cp = []
     for t in range(ng):
-        j = g_at(t)
+        j = g_at(t) if t < ng - 1 else g
 
         def one_belief(r, carry):
             b = j * own_rows + r
@@ -406,6 +420,12 @@
             )
             cp.start()
             rs_cp.append(cp)
+        if t == ng // 2 - 1:
+            for n, (source, target) in enumerate(((before, after), (after, before))):
+                ty_cp[n].wait_recv()
+                part_y = pl.ds(direct + source * per_y + n * (per_y // 2), per_y // 2)
+                ty_cp.append(trans_share(part_y, 2 + n, target))
+                ty_cp[-1].start()
 
     for cp in tot_cp:
         cp.wait_recv()
@@ -441,11 +461,7 @@
 
     def spread_owner(j):
         rows = pl.ds(pl.multiple_of(j * own_rows, own_rows), own_rows)
-        half = j // (ng // 2)
-        high_rows = pl.ds(pl.multiple_of((half * (ng // 2) + j) * own_rows, own_rows), own_rows)
-        low_rows = pl.ds(
-            pl.multiple_of((half * (ng // 2) + j) * own_rows + bel // 2, own_rows), own_rows
-        )
+        low_rows = pl.ds(pl.multiple_of(bel + j * own_rows, own_rows), own_rows)
         w_scale[rows, :] = jnp.broadcast_to(
             scale_of(w_all[j, own_rows : own_rows + 1, :]), (own_rows, width)
         )[:, :qwidth]
@@ -462,14 +478,14 @@
             for h in range(halves):
                 high, low = pieces[h]
                 cols = slice(a * width + h * LANES, a * width + (h + 1) * LANES)
-                spread[high_rows, cols] = jnp.where(hot, high, jnp.zeros_like(high))
+                spread[rows, cols] = jnp.where(hot, high, jnp.zeros_like(high))
                 spread[low_rows, cols] = jnp.where(hot, low, jnp.zeros_like(low))
 
     spread_owner(g)
     own_t.wait()
     for cp in t_cp:
         cp.wait_recv()
-    for cp in ty_cp:
+    for cp in ty_cp[2:]:
         cp.wait_recv()
 
     def total_action(a, carry):
@@ -490,18 +506,13 @@
 
     for t in range(ng - 1):
         w_cp[t].wait_recv()
-        spread_owner(lax.rem(g + ng - 1 - t, ng))
-    half_bel = bel // 2
-    group = nz // 2
-
-    def future_half(half):
-        rows = pl.ds(pl.multiple_of(half * half_bel, half_bel), half_bel)
-        both = jnp.dot(
-            spread[pl.ds(pl.multiple_of(half * bel, bel), bel), :],
-            t_blk[...].reshape(actions * width, qwidth),
-            preferred_element_type=jnp.float32,
-        )
-        fut[rows, :] = (256.0 * both[:half_bel] + both[half_bel:]) * w_scale[rows, :]
+        spread_owner(g_from(t))
+    both = jnp.dot(
+        spread[...],
+        t_blk[...].reshape(actions * width, qwidth),
+        preferred_element_type=jnp.float32,
+    )
+    fut[...] = (256.0 * both[:bel] + both[bel:]) * w_scale[...]
 
     def send_future(j, t):
         rows = pl.ds(pl.multiple_of(j * z_rows, z_rows), z_rows)
@@ -521,14 +532,8 @@
         f_cp.append(cp)
 
     f_cp = []
-    z_half = z // group
-    far_half = 1 - z_half
-    future_half(far_half)
-    for n in range(group):
-        send_future(far_half * group + lax.rem(z + n, group), n)
-    future_half(z_half)
-    for n in range(1, group):
-        send_future(z_half * group + lax.rem(z + n, group), group - 1 + n)
+    for t in far_first(nz):
+        send_future(z_at(t), t)
     own_rew.wait()
     for cp in f_cp:
         cp.wait_recv()
@@ -570,7 +575,7 @@
     out_ref[:, q_cols] = fin[g]
     for cp in o_cp:
         cp.wait_recv()
-    for cp in ob_cp + pk_cp + al_cp + share_cp + ts_cp + ty_cp + t_cp + relay_cp + tot_cp + rs_cp + w_cp + f_cp + tt_cp + o_cp:
+    for cp in ob_cp + pk_cp + al_cp[0] + al_cp[1] + share_cp + ts_cp + ty_cp + t_cp + relay_cp + tot_cp + rs_cp + w_cp + f_cp + tt_cp + o_cp:
         cp.wait_send()
 
 
@@ -620,20 +625,20 @@
         dma((5 + nz * obs_local,)),
         dma((nz - 1,)),
         dma((nz - 1,)),
+        dma((2, 2)),
+        dma((2, 2)),
         dma((2,)),
         dma((2,)),
-        dma((2,)),
-        dma((2,)),
+        dma((6,)),
+        dma((6,)),
+        dma((nz - 1,)),
+        dma((nz - 1,)),
+        dma((ng - 1,)),
+        dma((ng - 1,)),
+        dma((ng - 1,)),
+        dma((ng - 1,)),
         dma((4,)),
         dma((4,)),
-        dma((nz - 1,)),
-        dma((nz - 1,)),
-        dma((ng - 1,)),
-        dma((ng - 1,)),
-        dma((ng - 1,)),
-        dma((ng - 1,)),
-        dma((ny - 1,)),
-        dma((ny - 1,)),
         dma((ng - 1,)),
         dma((ng - 1,)),
         dma((ng - 1,)),

time: 57.2 us -> 58.1 us (1.016)
  Pallas kernels: 54.2 us -> 55.2 us
    pallas_call x1, Pallas kernels: 54.2 us -> 55.2 us  [body(): pl.pallas_call(functools.partial(kernel, dims), out_shape=jax.ShapeDtypeS...]
where the time goes in v5:
time: 58.1 us; the launch traced here: 58 us
  Pallas kernels  55.2 us (95%)
  local copies, waits for them, and re-layouts  2.72 us (5%)
    pallas_call x1, Pallas kernels, body(): pl.pallas_call(functools.partial(kernel, dims), out_shape=jax.ShapeDtypeS...  55.2 us
    unnamed x1, local copies, waits for them, and re-layouts  1.47 us
    reshape x1, local copies, waits for them, and re-layouts, body(): chosen_action.reshape(1, bel)  1.24 us

profile of v5, /device:TPU:1, one launch (start us, length us, event | category | flops | bytes accessed | tf_op | source)
XLA Modules:
  0.0 58.0 jit_solution(14288714791638759568)
XLA Ops:
  0.0 1.2 %reshape.3.act_row = s32[1,384]{1,0:T(1,128)} reshape(s32[384]{0:T(512)} %act_s.1) | data formatting | bytes 3072 | tf_op jit(solution)/shard_map/reshape | solution.py:675
  1.2 55.2 %backup.1 = f32[6,2048]{1,0:T(8,128)} custom-call(s32[384]{0:T(512)} %act_s.1, s32[1,384]{1,0:T(1,128)} %reshape.3.act_row, s32[16,4,384]{2,1,0:T(4,128)} %bitcast.1, bf16[512,2048]{1,0:T(8,128)(2,1)} %alpha_hbm.1, bf16[16,32,2048]{2,1,0:T(8,128)(2,1)} %trans_hbm.1, f32[4,16,2048]{2,1,0:T(8,128)} %obs_hbm.1, f32[16,2048]{1,0:T(8,128)} %rew_hbm.1), custom_call_target="tpu_custom_call" | custom-call | tf_op jit(solution)/shard_map/backup/pallas_call | solution.py:655
  56.5 1.5 %copy.8 = f32[6,2048]{1,0:T(8,128)} copy(f32[6,2048]{1,0:T(8,128)} %backup.1) | data formatting | bytes 98304

commit v6 on v5

--- a/solution.py
+++ b/solution.py
@@ -24,14 +24,14 @@
     level = jnp.ceil(32.0 * jnp.log(jnp.maximum(largest, 1e-30) * (1.0 / 32760.0)))
     inverse = jnp.exp(level * (-1.0 / 32.0))
     coded = [
-        jnp.clip(jnp.round(v * inverse), -32767.0, 32767.0).astype(jnp.int32).astype(jnp.int16)
+        jnp.clip(jnp.round(v * inverse), -32767.0, 32767.0).astype(jnp.int32)
         for v in values
     ]
-    return coded, jnp.broadcast_to(level, (8, LANES)).astype(jnp.int32).astype(jnp.int16)
+    return coded, jnp.broadcast_to(level, (8, LANES)).astype(jnp.int32)
 
 
 def scale_of(level):
-    return jnp.exp(level.astype(jnp.int32).astype(jnp.float32) * (1.0 / 32.0))
+    return jnp.exp(level * (1.0 / 32.0))
 
 
 def far_first(n):
@@ -53,6 +53,7 @@
     obs_hbm,
     rew_hbm,
     out_ref,
+    rew_ref,
     al_bf,
     al_rows,
     act_i,
@@ -78,7 +79,7 @@
     tt_own,
     tt_buf,
     rew_v,
-    fin,
+    tt_all,
     local_sem,
     pk_send,
     pk_recv,
@@ -106,8 +107,6 @@
     f_recv,
     tt_send,
     tt_recv,
-    o_send,
-    o_recv,
 ):
     ny, nz, nx, nc = dims
     ng = nx * nc
@@ -122,7 +121,7 @@
     half_y = rows_y // nc
     obs_local = obs_hbm.shape[0]
     t_rows = trans_hbm.shape[1]
-    last = fin.shape[1]
+    last = out_ref.shape[0]
     per_y = actions // (2 * ny)
     direct = actions - per_y * ny
 
@@ -180,7 +179,7 @@
     own_ts = pltpu.make_async_copy(
         trans_hbm.at[mine, :, q_cols], t_blk.at[mine, g_rows, :], local_sem.at[0]
     )
-    own_rew = pltpu.make_async_copy(rew_hbm.at[:, q_cols], rew_v, local_sem.at[4])
+    own_rew = pltpu.make_async_copy(rew_hbm, rew_v, local_sem.at[4])
     own_ob.start()
     own_al.start()
     own_t.start()
@@ -343,23 +342,6 @@
     for t, source in enumerate((before, after)):
         al_cp[t][1].wait_recv()
         share(source, quarters[1 - t])
-    own_ts.wait()
-    for cp in ts_cp:
-        cp.wait_recv()
-
-    def trans_share(which, n, target):
-        return pltpu.make_async_remote_copy(
-            t_blk.at[which],
-            t_blk.at[which],
-            ty_send.at[n],
-            ty_recv.at[n],
-            device_id={"bel": target},
-            device_id_type=MESH,
-        )
-
-    ty_cp = [trans_share(mine, 0, after), trans_share(mine, 1, before)]
-    for cp in ty_cp:
-        cp.start()
     for source in (before, after):
         spread_alpha(source, c * half_y, half_y)
     for t in range(2):
@@ -380,6 +362,23 @@
     for cp in tot_cp:
         cp.start()
 
+    own_ts.wait()
+    for cp in ts_cp:
+        cp.wait_recv()
+
+    def trans_share(which, n, target):
+        return pltpu.make_async_remote_copy(
+            t_blk.at[which],
+            t_blk.at[which],
+            ty_send.at[n],
+            ty_recv.at[n],
+            device_id={"bel": target},
+            device_id_type=MESH,
+        )
+
+    ty_cp = [trans_share(mine, 0, after), trans_share(mine, 1, before)]
+    for cp in ty_cp:
+        cp.start()
     other = (1 - c) * half_y
     for cp, (source, n) in zip(
         share_cp, ((before, 0), (after, 1), (before, 1), (after, 0), (across, 0), (across, 1))
@@ -447,8 +446,8 @@
     coded, level = to_codes(values)
     for h in range(halves):
         cols = slice(h * LANES, (h + 1) * LANES)
-        w_all[g, :own_rows, cols] = coded[h]
-        w_all[g, own_rows:, cols] = level
+        w_all[g, :own_rows, cols] = coded[h].astype(jnp.int16)
+        w_all[g, own_rows:, cols] = level.astype(jnp.int16)
 
     w_cp = [
         pltpu.make_async_remote_copy(
@@ -463,7 +462,7 @@
         rows = pl.ds(pl.multiple_of(j * own_rows, own_rows), own_rows)
         low_rows = pl.ds(pl.multiple_of(bel + j * own_rows, own_rows), own_rows)
         w_scale[rows, :] = jnp.broadcast_to(
-            scale_of(w_all[j, own_rows : own_rows + 1, :]), (own_rows, width)
+            scale_of(w_all[j, own_rows : own_rows + 1, :].astype(jnp.int32).astype(jnp.float32)), (own_rows, width)
         )[:, :qwidth]
         act = act_b[rows, :]
         pieces = []
@@ -516,66 +515,68 @@
 
     def send_future(j, t):
         rows = pl.ds(pl.multiple_of(j * z_rows, z_rows), z_rows)
-        (coded,), level = to_codes([fut[rows, :]])
-        fut_q[j, :z_rows, :] = coded
+        act = act_i[rows, :]
+        values = []
         for h in range(qwidth // LANES):
-            fut_q[j, z_rows:, h * LANES : (h + 1) * LANES] = level
-        cp = pltpu.make_async_remote_copy(
-            fut_q.at[j],
-            f_buf.at[t],
-            f_send.at[t],
-            f_recv.at[t],
-            device_id={"obs_0": j},
-            device_id_type=MESH,
-        )
-        cp.start()
-        f_cp.append(cp)
-
+            cols = slice(h * LANES, (h + 1) * LANES)
+            divisor = jnp.ones((z_rows, LANES), jnp.float32)
+            for a in range(actions):
+                divisor = jnp.where(act == a, tt_all[a : a + 1, cols], divisor)
+            values.append(fut[rows, cols] / divisor)
+        coded, level = to_codes(values)
+        for h, code in enumerate(coded):
+            cols = slice(h * LANES, (h + 1) * LANES)
+            for n in range(ng):
+                piece = jnp.concatenate([code[n * last : (n + 1) * last], level[: 8 - last]], axis=0)
+                fut_q[t + 1, n, :, cols] = piece.astype(jnp.int16)
+        for u in range(-1, ng - 1):
+            if t < 0 and u < 0:
+                continue
+            n = g if u < 0 else g_at(u)
+            cp = pltpu.make_async_remote_copy(
+                fut_q.at[t + 1, n],
+                f_buf.at[t + 1, u + 1],
+                f_send.at[t + 1, u + 1],
+                f_recv.at[t + 1, u + 1],
+                device_id={"obs_0": j, "obs_1": n // nc, "obs_2": lax.rem(n, nc)},
+                device_id_type=MESH,
+            )
+            cp.start()
+            f_cp.append(cp)
+
+    for cp in tt_cp:
+        cp.wait_recv()
+    total = tt_own[...]
+    for t in range(nz - 1):
+        total = total + tt_buf[t]
+    tt_all[...] = total
     f_cp = []
     for t in far_first(nz):
         send_future(z_at(t), t)
+    send_future(z, -1)
     own_rew.wait()
+    for r in range(last):
+        rew_ref[r : r + 1, :] = rew_v[pl.ds(act_s[(z * ng + g) * last + r], 1), :]
     for cp in f_cp:
         cp.wait_recv()
-    for cp in tt_cp:
-        cp.wait_recv()
-    z_start = pl.multiple_of(z * z_rows, z_rows)
-    act_z = act_i[pl.ds(z_start, z_rows), :]
-    for h in range(qwidth // LANES):
-        cols = slice(h * LANES, (h + 1) * LANES)
-        total = tt_own[:, cols]
-        for t in range(nz - 1):
-            total = total + tt_buf[t, :, cols]
-        future = fut[pl.ds(z_start, z_rows), cols]
-        for t in range(nz - 1):
-            piece = f_buf[t, :z_rows, cols].astype(jnp.int32).astype(jnp.float32)
-            future = future + piece * scale_of(f_buf[t, z_rows : z_rows + 1, cols])
-        divisor = jnp.ones((z_rows, LANES), jnp.float32)
-        reward = jnp.zeros((z_rows, LANES), jnp.float32)
-        for a in range(actions):
-            hot = act_z == a
-            divisor = jnp.where(hot, total[a : a + 1, :], divisor)
-            reward = jnp.where(hot, rew_v[a : a + 1, cols], reward)
-        result = reward + DISCOUNT * (future / divisor)
-        for n in range(ng):
-            fin[n, :, cols] = result[n * last : (n + 1) * last, :]
-    o_cp = [
-        pltpu.make_async_remote_copy(
-            fin.at[g_at(t)],
-            out_ref.at[:, q_cols],
-            o_send.at[t],
-            o_recv.at[t],
-            device_id=to_g(t),
-            device_id_type=MESH,
-        )
-        for t in range(ng - 1)
-    ]
-    for cp in o_cp:
-        cp.start()
-    out_ref[:, q_cols] = fin[g]
-    for cp in o_cp:
-        cp.wait_recv()
-    for cp in ob_cp + pk_cp + al_cp[0] + al_cp[1] + share_cp + ts_cp + ty_cp + t_cp + relay_cp + tot_cp + rs_cp + w_cp + f_cp + tt_cp + o_cp:
+
+    def add_pieces(u, at, read):
+        for h in range(qwidth // LANES):
+            cols = slice(h * LANES, (h + 1) * LANES)
+            future = None
+            for t in range(nz):
+                piece = read(t, cols)
+                term = piece * scale_of(piece[last : last + 1])
+                future = term if future is None else future + term
+            out_ref[:, pl.ds(pl.multiple_of(at * qwidth + h * LANES, LANES), LANES)] = future[:last]
+
+    for u in range(ng):
+        def read(t, cols):
+            piece = fut_q[0, g, :, cols] if u == 0 and t == 0 else f_buf[t, u, :, cols]
+            return piece.astype(jnp.int32).astype(jnp.float32)
+
+        add_pieces(u, g if u == 0 else g_from(u - 1), read)
+    for cp in ob_cp + pk_cp + al_cp[0] + al_cp[1] + share_cp + ts_cp + ty_cp + t_cp + relay_cp + tot_cp + rs_cp + w_cp + f_cp + tt_cp:
         cp.wait_send()
 
 
@@ -616,12 +617,12 @@
         pltpu.VMEM((2 * bel, actions * width), b16),
         pltpu.VMEM((bel, qwidth), f32),
         pltpu.VMEM((bel, qwidth), f32),
-        pltpu.VMEM((nz, z_rows + 8, qwidth), jnp.int16),
-        pltpu.VMEM((nz - 1, z_rows + 8, qwidth), jnp.int16),
+        pltpu.VMEM((nz, ng, 8, qwidth), jnp.int16),
+        pltpu.VMEM((nz, ng, 8, qwidth), jnp.int16),
         pltpu.VMEM((actions, qwidth), f32),
         pltpu.VMEM((nz - 1, actions, qwidth), f32),
+        pltpu.VMEM((actions, states), f32),
         pltpu.VMEM((actions, qwidth), f32),
-        pltpu.VMEM((ng, bel // (nz * ng), qwidth), f32),
         dma((5 + nz * obs_local,)),
         dma((nz - 1,)),
         dma((nz - 1,)),
@@ -645,16 +646,15 @@
         dma((ng - 1,)),
         dma((ng - 1,)),
         dma((ng - 1,)),
+        dma((nz, ng)),
+        dma((nz, ng)),
         dma((nz - 1,)),
         dma((nz - 1,)),
-        dma((nz - 1,)),
-        dma((nz - 1,)),
-        dma((ng - 1,)),
-        dma((ng - 1,)),
-    ]
-    return pl.pallas_call(
+    ]
+    rows = jax.ShapeDtypeStruct((bel // (nz * ng), states), f32)
+    future, reward = pl.pallas_call(
         functools.partial(kernel, dims),
-        out_shape=jax.ShapeDtypeStruct((bel // (nz * ng), states), f32),
+        out_shape=(rows, rows),
         in_specs=[
             pl.BlockSpec(memory_space=pltpu.SMEM),
             vmem,
@@ -664,7 +664,7 @@
             hbm,
             hbm,
         ],
-        out_specs=vmem,
+        out_specs=(vmem, vmem),
         scratch_shapes=scratch,
         compiler_params=pltpu.CompilerParams(
             collective_id=0, has_side_effects=True, vmem_limit_bytes=60 * 1024 * 1024
@@ -679,6 +679,7 @@
         obs_weights,
         rewards,
     )
+    return reward + DISCOUNT * future
 
 
 def solution(mesh):

time: 58.1 us -> 58.4 us (level)
  other arithmetic: 0 us -> 1.51 us
  local copies, waits for them, and re-layouts: 2.72 us -> 1.24 us
    add x0 -> x1, other arithmetic: none -> 1.51 us  [body(): return reward + DISCOUNT * future]
    unnamed x1 -> x0, local copies, waits for them, and re-layouts: 1.47 us -> none
where the time goes in v6:
time: 58.4 us; the launch traced here: 58.2 us
  Pallas kernels  55.4 us (95%)
  other arithmetic  1.51 us (3%)
  local copies, waits for them, and re-layouts  1.24 us (2%)
    pallas_call x1, Pallas kernels, body(): pl.pallas_call(functools.partial(kernel, dims), out_shape=(rows, rows), i...  55.4 us
    add x1, other arithmetic, body(): return reward + DISCOUNT * future  1.51 us
    reshape x1, local copies, waits for them, and re-layouts, body(): chosen_action.reshape(1, bel)  1.24 us

profile of v6, /device:TPU:1, one launch (start us, length us, event | category | flops | bytes accessed | tf_op | source)
XLA Modules:
  0.0 58.2 jit_solution(9817157011051421421)
XLA Ops:
  0.0 1.2 %reshape.3.act_row = s32[1,384]{1,0:T(1,128)} reshape(s32[384]{0:T(512)} %act_s.1) | data formatting | bytes 3072 | tf_op jit(solution)/shard_map/reshape | solution.py:675
  1.2 55.4 %backup.1 = (f32[6,2048]{1,0:T(8,128)}, f32[6,2048]{1,0:T(8,128)}) custom-call(s32[384]{0:T(512)} %act_s.1, s32[1,384]{1,0:T(1,128)} %reshape.3.act_row, s32[16,4,384]{2,1,0:T(4,128)} %bitcast.1, bf16[512,2048]{1,0:T(8,128)(2,1)} %alpha_hbm.1, bf16[16,32,2048]{2,1,0:T(8,128)(2,1)} %trans_hbm.1, f32[4,16,2048]{2,1,0:T(8,128)} %obs_hbm.1, f32[16,2048]{1,0:T(8,128)} %rew_hbm.1), custom_call_target="tpu_custom_call" | custom-call | tf_op jit(solution)/shard_map/backup/pallas_call | solution.py:655
  56.7 1.5 %multiply_add_fusion = f32[6,2048]{1,0:T(8,128)} fusion(f32[6,2048]{1,0:T(8,128)} %get-tuple-element.7, f32[6,2048]{1,0:T(8,128)} %get-tuple-element.8), kind=kLoop, calls=%fused_computation | loop fusion | flops 24576 | bytes 147456 | tf_op jit(solution)/shard_map/add | solution.py:682

commit v7 on v6

--- a/solution.py
+++ b/solution.py
@@ -11,6 +11,7 @@
 OBS = ("obs_0", "obs_1", "obs_2")
 BEL_OBS = ("bel", "obs_0", "obs_1", "obs_2")
 LANES = 128
+PIECE = 16
 DISCOUNT = 0.95
 CODE_SCALE = 14114.0
 CODE_SHIFT = 2.302585093 * CODE_SCALE
@@ -122,6 +123,7 @@
     obs_local = obs_hbm.shape[0]
     t_rows = trans_hbm.shape[1]
     last = out_ref.shape[0]
+    used = last * (qwidth // LANES)
     per_y = actions // (2 * ny)
     direct = actions - per_y * ny
 
@@ -376,7 +378,7 @@
             device_id_type=MESH,
         )
 
-    ty_cp = [trans_share(mine, 0, after), trans_share(mine, 1, before)]
+    ty_cp = [trans_share(mine, n, to) for n, to in enumerate((across, after, before))]
     for cp in ty_cp:
         cp.start()
     other = (1 - c) * half_y
@@ -419,12 +421,6 @@
             )
             cp.start()
             rs_cp.append(cp)
-        if t == ng // 2 - 1:
-            for n, (source, target) in enumerate(((before, after), (after, before))):
-                ty_cp[n].wait_recv()
-                part_y = pl.ds(direct + source * per_y + n * (per_y // 2), per_y // 2)
-                ty_cp.append(trans_share(part_y, 2 + n, target))
-                ty_cp[-1].start()
 
     for cp in tot_cp:
         cp.wait_recv()
@@ -484,7 +480,7 @@
     own_t.wait()
     for cp in t_cp:
         cp.wait_recv()
-    for cp in ty_cp[2:]:
+    for cp in ty_cp:
         cp.wait_recv()
 
     def total_action(a, carry):
@@ -524,18 +520,17 @@
                 divisor = jnp.where(act == a, tt_all[a : a + 1, cols], divisor)
             values.append(fut[rows, cols] / divisor)
         coded, level = to_codes(values)
-        for h, code in enumerate(coded):
-            cols = slice(h * LANES, (h + 1) * LANES)
-            for n in range(ng):
-                piece = jnp.concatenate([code[n * last : (n + 1) * last], level[: 8 - last]], axis=0)
-                fut_q[t + 1, n, :, cols] = piece.astype(jnp.int16)
+        for n in range(ng):
+            parts = [code[n * last : (n + 1) * last] for code in coded]
+            piece = jnp.concatenate(parts + [level[: PIECE - used]], axis=0)
+            fut_q[t + 1, n] = piece.astype(jnp.int16)
         for u in range(-1, ng - 1):
             if t < 0 and u < 0:
                 continue
             n = g if u < 0 else g_at(u)
             cp = pltpu.make_async_remote_copy(
-                fut_q.at[t + 1, n],
-                f_buf.at[t + 1, u + 1],
+                fut_q.at[t + 1, n, pl.ds(0, used + 2)],
+                f_buf.at[t + 1, u + 1, pl.ds(0, used + 2)],
                 f_send.at[t + 1, u + 1],
                 f_recv.at[t + 1, u + 1],
                 device_id={"obs_0": j, "obs_1": n // nc, "obs_2": lax.rem(n, nc)},
@@ -560,22 +555,18 @@
     for cp in f_cp:
         cp.wait_recv()
 
-    def add_pieces(u, at, read):
+    for u in range(ng):
+        at = g if u == 0 else g_from(u - 1)
+        future = None
+        for t in range(nz):
+            codes = fut_q[0, g] if u == 0 and t == 0 else f_buf[t, u]
+            codes = codes.astype(jnp.int32).astype(jnp.float32)
+            term = codes * scale_of(codes[used : used + 1])
+            future = term if future is None else future + term
         for h in range(qwidth // LANES):
-            cols = slice(h * LANES, (h + 1) * LANES)
-            future = None
-            for t in range(nz):
-                piece = read(t, cols)
-                term = piece * scale_of(piece[last : last + 1])
-                future = term if future is None else future + term
-            out_ref[:, pl.ds(pl.multiple_of(at * qwidth + h * LANES, LANES), LANES)] = future[:last]
-
-    for u in range(ng):
-        def read(t, cols):
-            piece = fut_q[0, g, :, cols] if u == 0 and t == 0 else f_buf[t, u, :, cols]
-            return piece.astype(jnp.int32).astype(jnp.float32)
-
-        add_pieces(u, g if u == 0 else g_from(u - 1), read)
+            out_ref[:, pl.ds(pl.multiple_of(at * qwidth + h * LANES, LANES), LANES)] = future[
+                h * last : (h + 1) * last
+            ]
     for cp in ob_cp + pk_cp + al_cp[0] + al_cp[1] + share_cp + ts_cp + ty_cp + t_cp + relay_cp + tot_cp + rs_cp + w_cp + f_cp + tt_cp:
         cp.wait_send()
 
@@ -617,8 +608,8 @@
         pltpu.VMEM((2 * bel, actions * width), b16),
         pltpu.VMEM((bel, qwidth), f32),
         pltpu.VMEM((bel, qwidth), f32),
-        pltpu.VMEM((nz, ng, 8, qwidth), jnp.int16),
-        pltpu.VMEM((nz, ng, 8, qwidth), jnp.int16),
+        pltpu.VMEM((nz, ng, PIECE, LANES), jnp.int16),
+        pltpu.VMEM((nz, ng, PIECE, LANES), jnp.int16),
         pltpu.VMEM((actions, qwidth), f32),
         pltpu.VMEM((nz - 1, actions, qwidth), f32),
         pltpu.VMEM((actions, states), f32),
@@ -638,8 +629,8 @@
         dma((ng - 1,)),
         dma((ng - 1,)),
         dma((ng - 1,)),
-        dma((4,)),
-        dma((4,)),
+        dma((ny - 1,)),
+        dma((ny - 1,)),
         dma((ng - 1,)),
         dma((ng - 1,)),
         dma((ng - 1,)),
@@ -651,7 +642,7 @@
         dma((nz - 1,)),
         dma((nz - 1,)),
     ]
-    rows = jax.ShapeDtypeStruct((bel // (nz * ng), states), f32)
+    rows = pltpu.VMEM((bel // (nz * ng), states), f32)
     future, reward = pl.pallas_call(
         functools.partial(kernel, dims),
         out_shape=(rows, rows),

time: 58.4 us -> 56.2 us (0.962)
  Pallas kernels: 55.4 us -> 54.1 us
  other arithmetic: 1.51 us -> 0.64 us
    pallas_call x1, Pallas kernels: 55.4 us -> 54.1 us  [body(): pl.pallas_call(functools.partial(kernel, dims), out_shape=(rows, rows), i...]
    add x1, other arithmetic: 1.51 us -> 0.64 us  [body(): return reward + DISCOUNT * future]
where the time goes in v7:
time: 56.2 us; the launch traced here: 56 us
  Pallas kernels  54.1 us (96%)
  local copies, waits for them, and re-layouts  1.24 us (2%)
  other arithmetic  0.64 us (1%)
    pallas_call x1, Pallas kernels, body(): pl.pallas_call(functools.partial(kernel, dims), out_shape=(rows, rows), i...  54.1 us
    reshape x1, local copies, waits for them, and re-layouts, body(): chosen_action.reshape(1, bel)  1.24 us

profile of v7, /device:TPU:1, one launch (start us, length us, event | category | flops | bytes accessed | tf_op | source)
XLA Modules:
  0.0 56.0 jit_solution(14204196440253696686)
XLA Ops:
  0.0 1.2 %reshape.3.act_row = s32[1,384]{1,0:T(1,128)} reshape(s32[384]{0:T(512)} %act_s.1) | data formatting | bytes 3072 | tf_op jit(solution)/shard_map/reshape | solution.py:666
  1.2 54.1 %backup.1 = (f32[6,2048]{1,0:T(8,128)S(1)}, f32[6,2048]{1,0:T(8,128)S(1)}) custom-call(s32[384]{0:T(512)} %act_s.1, s32[1,384]{1,0:T(1,128)} %reshape.3.act_row, s32[16,4,384]{2,1,0:T(4,128)} %bitcast.1, bf16[512,2048]{1,0:T(8,128)(2,1)} %alpha_hbm.1, bf16[16,32,2048]{2,1,0:T(8,128)(2,1)} %trans_hbm.1, f32[4,16,2048]{2,1,0:T(8,128)} %obs_hbm.1, ...), custom_call_target="tpu_custom_call" | custom-call | tf_op jit(solution)/shard_map/backup/pallas_call | solution.py:646
  55.4 0.6 %multiply_add_fusion = f32[6,2048]{1,0:T(8,128)} fusion(f32[6,2048]{1,0:T(8,128)S(1)} %get-tuple-element.7, f32[6,2048]{1,0:T(8,128)S(1)} %get-tuple-element.8), kind=kLoop, calls=%fused_computation | loop fusion | flops 24576 | bytes 147456 | tf_op jit(solution)/shard_map/add | solution.py:673

commit v8 on v7

--- a/solution.py
+++ b/solution.py
@@ -46,9 +46,8 @@
 
 def kernel(
     dims,
-    act_s,
-    act_row,
-    idx_ref,
+    act_hbm,
+    idx_hbm,
     alpha_hbm,
     trans_hbm,
     obs_hbm,
@@ -57,6 +56,9 @@
     rew_ref,
     al_bf,
     al_rows,
+    act_s,
+    act_v,
+    idx_v,
     act_i,
     act_b,
     obs_v,
@@ -171,7 +173,7 @@
     z_cols = pl.ds(pl.multiple_of(z * width, width), width)
     q_cols = pl.ds(pl.multiple_of(g * qwidth, qwidth), qwidth)
 
-    own_al = pltpu.make_async_copy(alpha_hbm.at[:, z_cols], al_bf.at[y], local_sem.at[1])
+    own_al = pltpu.make_async_copy(alpha_hbm.at[:, z_cols], al_bf.at[y], local_sem.at[7])
     own_ob = pltpu.make_async_copy(obs_hbm, obs_v, local_sem.at[2])
     g_rows = pl.ds(pl.multiple_of(g * t_rows, t_rows), t_rows)
     mine = pl.ds(direct + y * per_y, per_y)
@@ -182,15 +184,25 @@
         trans_hbm.at[mine, :, q_cols], t_blk.at[mine, g_rows, :], local_sem.at[0]
     )
     own_rew = pltpu.make_async_copy(rew_hbm, rew_v, local_sem.at[4])
+    own_act = [
+        pltpu.make_async_copy(act_hbm, act_s, local_sem.at[1]),
+        pltpu.make_async_copy(act_hbm, act_v, local_sem.at[5]),
+        pltpu.make_async_copy(idx_hbm, idx_v, local_sem.at[6]),
+    ]
+    for cp in own_act:
+        cp.start()
     own_ob.start()
     own_al.start()
     own_t.start()
     own_ts.start()
     own_rew.start()
 
+    for cp in own_act:
+        cp.wait()
+    act_row = act_v[...].reshape(1, bel)
     picks = jnp.zeros((obs_local, bel), jnp.int32)
     for a in range(actions):
-        picks = jnp.where(act_row[...] == a, idx_ref[a] * halves, picks)
+        picks = jnp.where(act_row == a, idx_v[a] * halves, picks)
     for o in range(obs_local):
         pk_own[o] = picks[o : o + 1, :]
         pk_v[z, o] = picks[o : o + 1, :]
@@ -268,8 +280,6 @@
         ob_cp[t].start()
     for cp in ts_cp:
         cp.start()
-    for cp in t_cp:
-        cp.start()
 
     def spread_alpha(block, start, rows):
         def rows16(n, carry):
@@ -289,7 +299,7 @@
         cp.wait_recv()
     to_scalar = [
         [
-            pltpu.make_async_copy(pk_v.at[n, o], pk_s[n][o], local_sem.at[5 + n * obs_local + o])
+            pltpu.make_async_copy(pk_v.at[n, o], pk_s[n][o], local_sem.at[8 + n * obs_local + o])
             for o in range(obs_local)
         ]
         for n in range(nz)
@@ -344,12 +354,31 @@
     for t, source in enumerate((before, after)):
         al_cp[t][1].wait_recv()
         share(source, quarters[1 - t])
+    for cp in t_cp:
+        cp.start()
     for source in (before, after):
         spread_alpha(source, c * half_y, half_y)
     for t in range(2):
         relay_cp[t].wait_recv()
         share(across, quarters[t])
     spread_alpha(across, c * half_y, half_y)
+    own_ts.wait()
+    for cp in ts_cp:
+        cp.wait_recv()
+
+    def trans_share(which, n, target):
+        return pltpu.make_async_remote_copy(
+            t_blk.at[which],
+            t_blk.at[which],
+            ty_send.at[n],
+            ty_recv.at[n],
+            device_id={"bel": target},
+            device_id_type=MESH,
+        )
+
+    ty_cp = [trans_share(mine, n, to) for n, to in enumerate((across, after, before))]
+    for cp in ty_cp:
+        cp.start()
     for t in far_first(nz):
         ob_cp[t].wait_recv()
         decode(obs_all, lax.rem(z + nz - 1 - t, nz))
@@ -364,23 +393,6 @@
     for cp in tot_cp:
         cp.start()
 
-    own_ts.wait()
-    for cp in ts_cp:
-        cp.wait_recv()
-
-    def trans_share(which, n, target):
-        return pltpu.make_async_remote_copy(
-            t_blk.at[which],
-            t_blk.at[which],
-            ty_send.at[n],
-            ty_recv.at[n],
-            device_id={"bel": target},
-            device_id_type=MESH,
-        )
-
-    ty_cp = [trans_share(mine, n, to) for n, to in enumerate((across, after, before))]
-    for cp in ty_cp:
-        cp.start()
     other = (1 - c) * half_y
     for cp, (source, n) in zip(
         share_cp, ((before, 0), (after, 1), (before, 1), (after, 0), (across, 0), (across, 1))
@@ -590,6 +602,9 @@
     scratch = [
         pltpu.VMEM((ny, count // ny, width), b16),
         pltpu.VMEM((count * halves, LANES), f32),
+        pltpu.SMEM((bel,), i32),
+        pltpu.VMEM((bel,), i32),
+        pltpu.VMEM((actions, obs_local, bel), i32),
         pltpu.VMEM((bel, LANES), i32),
         pltpu.VMEM((bel, LANES), b16),
         pltpu.VMEM((obs_local, actions, states), f32),
@@ -614,7 +629,7 @@
         pltpu.VMEM((nz - 1, actions, qwidth), f32),
         pltpu.VMEM((actions, states), f32),
         pltpu.VMEM((actions, qwidth), f32),
-        dma((5 + nz * obs_local,)),
+        dma((8 + nz * obs_local,)),
         dma((nz - 1,)),
         dma((nz - 1,)),
         dma((2, 2)),
@@ -647,9 +662,8 @@
         functools.partial(kernel, dims),
         out_shape=(rows, rows),
         in_specs=[
-            pl.BlockSpec(memory_space=pltpu.SMEM),
-            vmem,
-            vmem,
+            hbm,
+            hbm,
             hbm,
             hbm,
             hbm,
@@ -663,7 +677,6 @@
         name="backup",
     )(
         chosen_action,
-        chosen_action.reshape(1, bel),
         jnp.transpose(chosen_idx, (1, 2, 0)),
         alpha_set,
         transitions,

time: 56.2 us -> 55.6 us (0.989)
  local copies, waits for them, and re-layouts: 1.24 us -> 0 us
  Pallas kernels: 54.1 us -> 54.9 us
    reshape x1 -> x0, local copies, waits for them, and re-layouts: 1.24 us -> none  [body(): chosen_action.reshape(1, bel)]
    pallas_call x1, Pallas kernels: 54.1 us -> 54.9 us  [body(): pl.pallas_call(functools.partial(kernel, dims), out_shape=(rows, rows), i...]
where the time goes in v8:
time: 55.6 us; the launch traced here: 55.5 us
  Pallas kernels  54.9 us (99%)
  other arithmetic  0.64 us (1%)
    pallas_call x1, Pallas kernels, body(): pl.pallas_call(functools.partial(kernel, dims), out_shape=(rows, rows), i...  54.9 us

profile of v8, /device:TPU:1, one launch (start us, length us, event | category | flops | bytes accessed | tf_op | source)
XLA Modules:
  0.0 55.5 jit_solution(5871415208867962595)
XLA Ops:
  0.0 54.9 %backup.1 = (f32[6,2048]{1,0:T(8,128)S(1)}, f32[6,2048]{1,0:T(8,128)S(1)}) custom-call(s32[384]{0:T(512)} %act_hbm.1, s32[16,4,384]{2,1,0:T(4,128)} %bitcast.1, bf16[512,2048]{1,0:T(8,128)(2,1)} %alpha_hbm.1, bf16[16,32,2048]{2,1,0:T(8,128)(2,1)} %trans_hbm.1, f32[4,16,2048]{2,1,0:T(8,128)} %obs_hbm.1, f32[16,2048]{1,0:T(8,128)} %rew_hbm.1), custom_call_target="tpu_custom_call" | custom-call | tf_op jit(solution)/shard_map/backup/pallas_call | solution.py:661
  54.9 0.6 %multiply_add_fusion = f32[6,2048]{1,0:T(8,128)} fusion(f32[6,2048]{1,0:T(8,128)S(1)} %get-tuple-element.7, f32[6,2048]{1,0:T(8,128)S(1)} %get-tuple-element.8), kind=kLoop, calls=%fused_computation | loop fusion | flops 24576 | bytes 147456 | tf_op jit(solution)/shard_map/add | solution.py:686

commit v9 on v8

--- a/solution.py
+++ b/solution.py
@@ -280,6 +280,8 @@
         ob_cp[t].start()
     for cp in ts_cp:
         cp.start()
+    for cp in t_cp:
+        cp.start()
 
     def spread_alpha(block, start, rows):
         def rows16(n, carry):
@@ -354,14 +356,32 @@
     for t, source in enumerate((before, after)):
         al_cp[t][1].wait_recv()
         share(source, quarters[1 - t])
-    for cp in t_cp:
-        cp.start()
     for source in (before, after):
         spread_alpha(source, c * half_y, half_y)
     for t in range(2):
         relay_cp[t].wait_recv()
         share(across, quarters[t])
     spread_alpha(across, c * half_y, half_y)
+    for t in far_first(nz):
+        ob_cp[t].wait_recv()
+        decode(obs_all, lax.rem(z + nz - 1 - t, nz))
+    for h in range(halves):
+        tot_own[h] = totals[h]
+    tot_cp = [
+        pltpu.make_async_remote_copy(
+            tot_own, tot_buf.at[t], tot_send.at[t], tot_recv.at[t], device_id=to_g(t), device_id_type=MESH
+        )
+        for t in range(ng - 1)
+    ]
+    for cp in tot_cp:
+        cp.start()
+
+    other = (1 - c) * half_y
+    for cp, (source, n) in zip(
+        share_cp, ((before, 0), (after, 1), (before, 1), (after, 0), (across, 0), (across, 1))
+    ):
+        cp.wait_recv()
+        spread_alpha(source, other + n * quarter, quarter)
     own_ts.wait()
     for cp in ts_cp:
         cp.wait_recv()
@@ -379,26 +399,6 @@
     ty_cp = [trans_share(mine, n, to) for n, to in enumerate((across, after, before))]
     for cp in ty_cp:
         cp.start()
-    for t in far_first(nz):
-        ob_cp[t].wait_recv()
-        decode(obs_all, lax.rem(z + nz - 1 - t, nz))
-    for h in range(halves):
-        tot_own[h] = totals[h]
-    tot_cp = [
-        pltpu.make_async_remote_copy(
-            tot_own, tot_buf.at[t], tot_send.at[t], tot_recv.at[t], device_id=to_g(t), device_id_type=MESH
-        )
-        for t in range(ng - 1)
-    ]
-    for cp in tot_cp:
-        cp.start()
-
-    other = (1 - c) * half_y
-    for cp, (source, n) in zip(
-        share_cp, ((before, 0), (after, 1), (before, 1), (after, 0), (across, 0), (across, 1))
-    ):
-        cp.wait_recv()
-        spread_alpha(source, other + n * quarter, quarter)
     for pair in to_scalar:
         for cp in pair:
             cp.wait()

time: 55.6 us -> 53.6 us (0.964)
  Pallas kernels: 54.9 us -> 52.8 us
    pallas_call x1, Pallas kernels: 54.9 us -> 52.8 us  [body(): pl.pallas_call(functools.partial(kernel, dims), out_shape=(rows, rows), i...]
where the time goes in v9:
time: 53.6 us; the launch traced here: 53.5 us
  Pallas kernels  52.8 us (99%)
  other arithmetic  0.64 us (1%)
    pallas_call x1, Pallas kernels, body(): pl.pallas_call(functools.partial(kernel, dims), out_shape=(rows, rows), i...  52.8 us

profile of v9, /device:TPU:1, one launch (start us, length us, event | category | flops | bytes accessed | tf_op | source)
XLA Modules:
  0.0 53.5 jit_solution(2095294337465785946)
XLA Ops:
  0.0 52.8 %backup.1 = (f32[6,2048]{1,0:T(8,128)S(1)}, f32[6,2048]{1,0:T(8,128)S(1)}) custom-call(s32[384]{0:T(512)} %act_hbm.1, s32[16,4,384]{2,1,0:T(4,128)} %bitcast.1, bf16[512,2048]{1,0:T(8,128)(2,1)} %alpha_hbm.1, bf16[16,32,2048]{2,1,0:T(8,128)(2,1)} %trans_hbm.1, f32[4,16,2048]{2,1,0:T(8,128)} %obs_hbm.1, f32[16,2048]{1,0:T(8,128)} %rew_hbm.1), custom_call_target="tpu_custom_call" | custom-call | tf_op jit(solution)/shard_map/backup/pallas_call | solution.py:661
  52.9 0.6 %multiply_add_fusion = f32[6,2048]{1,0:T(8,128)} fusion(f32[6,2048]{1,0:T(8,128)S(1)} %get-tuple-element.7, f32[6,2048]{1,0:T(8,128)S(1)} %get-tuple-element.8), kind=kLoop, calls=%fused_computation | loop fusion | flops 24576 | bytes 147456 | tf_op jit(solution)/shard_map/add | solution.py:686

commit v10 on v9

--- a/solution.py
+++ b/solution.py
@@ -79,6 +79,7 @@
     fut,
     fut_q,
     f_buf,
+    tt_share,
     tt_own,
     tt_buf,
     rew_v,
@@ -100,6 +101,8 @@
     ts_recv,
     ty_send,
     ty_recv,
+    tp_send,
+    tp_recv,
     tot_send,
     tot_recv,
     rs_send,
@@ -273,7 +276,20 @@
     for cp in pk_cp:
         cp.start()
     own_al.wait()
+    across = lax.rem(y + ny - 2, ny)
+    relay_cp = [
+        pltpu.make_async_remote_copy(
+            al_bf.at[y, quarters[n]],
+            al_bf.at[y, quarters[n]],
+            relay_send.at[n],
+            relay_recv.at[n],
+            device_id={"bel": across},
+            device_id_type=MESH,
+        )
+        for n in range(2)
+    ]
     for m in range(2):
+        relay_cp[m].start()
         for pair in al_cp:
             pair[m].start()
     for t in far_first(nz):
@@ -338,20 +354,8 @@
         share_cp.append(cp)
 
     before, after, across = (lax.rem(y + n, ny) for n in (ny - 1, 1, ny - 2))
-    relay_cp = []
-    for t, (source, target) in enumerate(((before, after), (after, before))):
+    for t, source in enumerate((before, after)):
         al_cp[t][0].wait_recv()
-        cp = pltpu.make_async_remote_copy(
-            al_bf.at[source, quarters[t]],
-            al_bf.at[source, quarters[t]],
-            relay_send.at[t],
-            relay_recv.at[t],
-            device_id={"bel": target},
-            device_id_type=MESH,
-        )
-        cp.start()
-        relay_cp.append(cp)
-    for t, source in enumerate((before, after)):
         share(source, quarters[t])
     for t, source in enumerate((before, after)):
         al_cp[t][1].wait_recv()
@@ -386,6 +390,25 @@
     for cp in ts_cp:
         cp.wait_recv()
 
+    def trans_total(a):
+        return jnp.sum(t_blk[a].astype(jnp.float32), axis=0, keepdims=True)
+
+    for n in range(per_y):
+        tt_share[y, n : n + 1, :] = trans_total(direct + y * per_y + n)
+    tp_cp = [
+        pltpu.make_async_remote_copy(
+            tt_share.at[y],
+            tt_share.at[y],
+            tp_send.at[n],
+            tp_recv.at[n],
+            device_id={"bel": to},
+            device_id_type=MESH,
+        )
+        for n, to in enumerate((across, after, before))
+    ]
+    for cp in tp_cp:
+        cp.start()
+
     def trans_share(which, n, target):
         return pltpu.make_async_remote_copy(
             t_blk.at[which],
@@ -492,16 +515,16 @@
     own_t.wait()
     for cp in t_cp:
         cp.wait_recv()
-    for cp in ty_cp:
-        cp.wait_recv()
 
     def total_action(a, carry):
-        tt_own[pl.ds(a, 1), :] = jnp.sum(
-            t_blk[a].astype(jnp.float32), axis=0, keepdims=True
-        )
+        tt_own[pl.ds(a, 1), :] = trans_total(a)
         return carry
 
-    lax.fori_loop(0, actions, total_action, 0)
+    lax.fori_loop(0, direct, total_action, 0)
+    for cp in tp_cp:
+        cp.wait_recv()
+    for n in range(ny):
+        tt_own[direct + n * per_y : direct + (n + 1) * per_y, :] = tt_share[n]
     tt_cp = [
         pltpu.make_async_remote_copy(
             tt_own, tt_buf.at[t], tt_send.at[t], tt_recv.at[t], device_id=to_z(t), device_id_type=MESH
@@ -514,6 +537,8 @@
     for t in range(ng - 1):
         w_cp[t].wait_recv()
         spread_owner(g_from(t))
+    for cp in ty_cp:
+        cp.wait_recv()
     both = jnp.dot(
         spread[...],
         t_blk[...].reshape(actions * width, qwidth),
@@ -579,7 +604,7 @@
             out_ref[:, pl.ds(pl.multiple_of(at * qwidth + h * LANES, LANES), LANES)] = future[
                 h * last : (h + 1) * last
             ]
-    for cp in ob_cp + pk_cp + al_cp[0] + al_cp[1] + share_cp + ts_cp + ty_cp + t_cp + relay_cp + tot_cp + rs_cp + w_cp + f_cp + tt_cp:
+    for cp in ob_cp + pk_cp + al_cp[0] + al_cp[1] + share_cp + ts_cp + tp_cp + ty_cp + t_cp + relay_cp + tot_cp + rs_cp + w_cp + f_cp + tt_cp:
         cp.wait_send()
 
 
@@ -625,6 +650,7 @@
         pltpu.VMEM((bel, qwidth), f32),
         pltpu.VMEM((nz, ng, PIECE, LANES), jnp.int16),
         pltpu.VMEM((nz, ng, PIECE, LANES), jnp.int16),
+        pltpu.VMEM((dims[0], actions // (2 * dims[0]), qwidth), f32),
         pltpu.VMEM((actions, qwidth), f32),
         pltpu.VMEM((nz - 1, actions, qwidth), f32),
         pltpu.VMEM((actions, states), f32),
@@ -644,6 +670,8 @@
         dma((ng - 1,)),
         dma((ng - 1,)),
         dma((ng - 1,)),
+        dma((ny - 1,)),
+        dma((ny - 1,)),
         dma((ny - 1,)),
         dma((ny - 1,)),
         dma((ng - 1,)),

time: 53.6 us -> 52 us (0.970)
  Pallas kernels: 52.8 us -> 51.2 us
    pallas_call x1, Pallas kernels: 52.8 us -> 51.2 us  [body(): pl.pallas_call(functools.partial(kernel, dims), out_shape=(rows, rows), i...]
where the time goes in v10:
time: 52 us; the launch traced here: 51.9 us
  Pallas kernels  51.2 us (98%)
  other arithmetic  0.64 us (1%)
    pallas_call x1, Pallas kernels, body(): pl.pallas_call(functools.partial(kernel, dims), out_shape=(rows, rows), i...  51.2 us

profile of v10, /device:TPU:1, one launch (start us, length us, event | category | flops | bytes accessed | tf_op | source)
XLA Modules:
  0.0 51.9 jit_solution(11067674193926696362)
XLA Ops:
  0.0 51.2 %backup.1 = (f32[6,2048]{1,0:T(8,128)S(1)}, f32[6,2048]{1,0:T(8,128)S(1)}) custom-call(s32[384]{0:T(512)} %act_hbm.1, s32[16,4,384]{2,1,0:T(4,128)} %bitcast.1, bf16[512,2048]{1,0:T(8,128)(2,1)} %alpha_hbm.1, bf16[16,32,2048]{2,1,0:T(8,128)(2,1)} %trans_hbm.1, f32[4,16,2048]{2,1,0:T(8,128)} %obs_hbm.1, f32[16,2048]{1,0:T(8,128)} %rew_hbm.1), custom_call_target="tpu_custom_call" | custom-call | tf_op jit(solution)/shard_map/backup/pallas_call | solution.py:689
  51.2 0.6 %multiply_add_fusion = f32[6,2048]{1,0:T(8,128)} fusion(f32[6,2048]{1,0:T(8,128)S(1)} %get-tuple-element.7, f32[6,2048]{1,0:T(8,128)S(1)} %get-tuple-element.8), kind=kLoop, calls=%fused_computation | loop fusion | flops 24576 | bytes 147456 | tf_op jit(solution)/shard_map/add | solution.py:714

commit v11 on v10

--- a/solution.py
+++ b/solution.py
@@ -69,6 +69,7 @@
     pk_v,
     pk_s,
     part,
+    sib_buf,
     rs_buf,
     tot_own,
     tot_buf,
@@ -210,12 +211,6 @@
         pk_own[o] = picks[o : o + 1, :]
         pk_v[z, o] = picks[o : o + 1, :]
 
-    def fill_action(b, carry):
-        act_i[pl.ds(b, 1), :] = jnp.full((1, LANES), act_s[b], jnp.int32)
-        return carry
-
-    lax.fori_loop(0, bel, fill_action, 0, unroll=8)
-    act_b[...] = act_i[...].astype(jnp.float32).astype(jnp.bfloat16)
     own_ob.wait()
     for n in range(nz):
         for o in range(obs_local):
@@ -313,18 +308,12 @@
 
     spread_alpha(y, 0, rows_y)
 
-    for cp in pk_cp:
-        cp.wait_recv()
-    to_scalar = [
-        [
-            pltpu.make_async_copy(pk_v.at[n, o], pk_s[n][o], local_sem.at[8 + n * obs_local + o])
-            for o in range(obs_local)
-        ]
-        for n in range(nz)
-    ]
-    for pair in to_scalar:
-        for cp in pair:
-            cp.start()
+    def fill_action(b, carry):
+        act_i[pl.ds(b, 1), :] = jnp.full((1, LANES), act_s[b], jnp.int32)
+        return carry
+
+    lax.fori_loop(0, bel, fill_action, 0, unroll=8)
+    act_b[...] = act_i[...].astype(jnp.float32).astype(jnp.bfloat16)
 
     totals = [jnp.zeros((actions, LANES), jnp.float32) for _ in range(halves)]
 
@@ -360,11 +349,23 @@
     for t, source in enumerate((before, after)):
         al_cp[t][1].wait_recv()
         share(source, quarters[1 - t])
-    for source in (before, after):
-        spread_alpha(source, c * half_y, half_y)
     for t in range(2):
         relay_cp[t].wait_recv()
         share(across, quarters[t])
+    for cp in pk_cp:
+        cp.wait_recv()
+    to_scalar = [
+        [
+            pltpu.make_async_copy(pk_v.at[n, o], pk_s[n][o], local_sem.at[8 + n * obs_local + o])
+            for o in range(obs_local)
+        ]
+        for n in range(nz)
+    ]
+    for pair in to_scalar:
+        for cp in pair:
+            cp.start()
+    for source in (before, after):
+        spread_alpha(source, c * half_y, half_y)
     spread_alpha(across, c * half_y, half_y)
     for t in far_first(nz):
         ob_cp[t].wait_recv()
@@ -426,9 +427,12 @@
         for cp in pair:
             cp.wait()
     rs_cp = []
-    for t in range(ng):
-        j = g_at(t) if t < ng - 1 else g
-
+    rows = own_rows * halves
+
+    def part_rows(j):
+        return pl.ds(pl.multiple_of(j * rows, rows), rows)
+
+    def weigh(j):
         def one_belief(r, carry):
             b = j * own_rows + r
             a = act_s[b]
@@ -444,22 +448,36 @@
             return carry
 
         lax.fori_loop(0, own_rows, one_belief, 0, unroll=4)
-        if t < ng - 1:
-            rows = own_rows * halves
-            cp = pltpu.make_async_remote_copy(
-                part.at[pl.ds(pl.multiple_of(j * rows, rows), rows), :],
-                rs_buf.at[t],
-                rs_send.at[t],
-                rs_recv.at[t],
-                device_id=to_g(t),
-                device_id_type=MESH,
-            )
-            cp.start()
-            rs_cp.append(cp)
-
+
+    def send_part(j, landing, n, to):
+        cp = pltpu.make_async_remote_copy(
+            part.at[part_rows(j), :],
+            landing,
+            rs_send.at[n],
+            rs_recv.at[n],
+            device_id=to,
+            device_id_type=MESH,
+        )
+        cp.start()
+        rs_cp.append(cp)
+
+    steps = sorted(range(1, nx), key=lambda d: -min(d, nx - d))
+    for n, d in enumerate(steps):
+        j = lax.rem(x + d, nx) * nc + (1 - c)
+        weigh(j)
+        send_part(j, sib_buf.at[n], n, {"obs_2": 1 - c})
+    for n, d in enumerate(steps):
+        j = lax.rem(x + d, nx) * nc + c
+        weigh(j)
+        rs_cp[n].wait_recv()
+        part[part_rows(j), :] = part[part_rows(j), :] + sib_buf[n]
+        send_part(j, rs_buf.at[n], nx - 1 + n, {"obs_1": lax.rem(x + d, nx)})
+    weigh(x * nc + (1 - c))
+    send_part(x * nc + (1 - c), rs_buf.at[nx - 1], ng - 2, {"obs_2": 1 - c})
+    weigh(g)
     for cp in tot_cp:
         cp.wait_recv()
-    for cp in rs_cp:
+    for cp in rs_cp[nx - 1 :]:
         cp.wait_recv()
     act_own = act_i[pl.ds(pl.multiple_of(g * own_rows, own_rows), own_rows), :]
     values = []
@@ -468,7 +486,7 @@
         for t in range(ng - 1):
             total = total + tot_buf[t, h]
         raw = part[pl.ds(g * own_rows * halves + h, own_rows, stride=halves), :]
-        for t in range(ng - 1):
+        for t in range(nx):
             raw = raw + rs_buf[t, pl.ds(h, own_rows, stride=halves), :]
         divisor = jnp.ones((own_rows, LANES), jnp.float32)
         for a in range(actions):
@@ -640,7 +658,8 @@
         pltpu.VMEM((nz, obs_local, 1, bel), i32),
         [[pltpu.SMEM((1, bel), i32) for _ in range(obs_local)] for _ in range(nz)],
         pltpu.VMEM((bel * halves, LANES), f32),
-        pltpu.VMEM((ng - 1, own_rows * halves, LANES), f32),
+        pltpu.VMEM((dims[2] - 1, own_rows * halves, LANES), f32),
+        pltpu.VMEM((dims[2], own_rows * halves, LANES), f32),
         pltpu.VMEM((halves, actions, LANES), f32),
         pltpu.VMEM((ng - 1, halves, actions, LANES), f32),
         pltpu.VMEM((ng, own_rows + 8, width), jnp.int16),

time: 52 us -> 50.5 us (0.971)
  Pallas kernels: 51.2 us -> 49.7 us
    pallas_call x1, Pallas kernels: 51.2 us -> 49.7 us  [body(): pl.pallas_call(functools.partial(kernel, dims), out_shape=(rows, rows), i...]
where the time goes in v11:
time: 50.5 us; the launch traced here: 50.4 us
  Pallas kernels  49.7 us (98%)
  other arithmetic  0.64 us (1%)
    pallas_call x1, Pallas kernels, body(): pl.pallas_call(functools.partial(kernel, dims), out_shape=(rows, rows), i...  49.7 us

profile of v11, /device:TPU:1, one launch (start us, length us, event | category | flops | bytes accessed | tf_op | source)
XLA Modules:
  0.0 50.4 jit_solution(1880193272190299936)
XLA Ops:
  0.0 49.7 %backup.1 = (f32[6,2048]{1,0:T(8,128)S(1)}, f32[6,2048]{1,0:T(8,128)S(1)}) custom-call(s32[384]{0:T(512)} %act_hbm.1, s32[16,4,384]{2,1,0:T(4,128)} %bitcast.1, bf16[512,2048]{1,0:T(8,128)(2,1)} %alpha_hbm.1, bf16[16,32,2048]{2,1,0:T(8,128)(2,1)} %trans_hbm.1, f32[4,16,2048]{2,1,0:T(8,128)} %obs_hbm.1, f32[16,2048]{1,0:T(8,128)} %rew_hbm.1), custom_call_target="tpu_custom_call" | custom-call | tf_op jit(solution)/shard_map/backup/pallas_call | solution.py:708
  49.7 0.6 %multiply_add_fusion = f32[6,2048]{1,0:T(8,128)} fusion(f32[6,2048]{1,0:T(8,128)S(1)} %get-tuple-element.7, f32[6,2048]{1,0:T(8,128)S(1)} %get-tuple-element.8), kind=kLoop, calls=%fused_computation | loop fusion | flops 24576 | bytes 147456 | tf_op jit(solution)/shard_map/add | solution.py:733

commit v12 on v11

--- a/solution.py
+++ b/solution.py
@@ -284,9 +284,10 @@
         for n in range(2)
     ]
     for m in range(2):
-        relay_cp[m].start()
         for pair in al_cp:
             pair[m].start()
+    for m in range(2):
+        relay_cp[m].start()
     for t in far_first(nz):
         ob_cp[t].start()
     for cp in ts_cp:
@@ -447,7 +448,7 @@
             )
             return carry
 
-        lax.fori_loop(0, own_rows, one_belief, 0, unroll=4)
+        lax.fori_loop(0, own_rows, one_belief, 0, unroll=8)
 
     def send_part(j, landing, n, to):
         cp = pltpu.make_async_remote_copy(

time: 50.5 us -> 49.9 us (0.988)
    pallas_call x1, Pallas kernels: 49.7 us -> 49.2 us  [body(): pl.pallas_call(functools.partial(kernel, dims), out_shape=(rows, rows), i...]
where the time goes in v12:
time: 49.9 us; the launch traced here: 49.8 us
  Pallas kernels  49.2 us (99%)
  other arithmetic  0.64 us (1%)
    pallas_call x1, Pallas kernels, body(): pl.pallas_call(functools.partial(kernel, dims), out_shape=(rows, rows), i...  49.2 us

profile of v12, /device:TPU:1, one launch (start us, length us, event | category | flops | bytes accessed | tf_op | source)
XLA Modules:
  0.0 49.8 jit_solution(15709399253088046495)
XLA Ops:
  0.0 49.2 %backup.1 = (f32[6,2048]{1,0:T(8,128)S(1)}, f32[6,2048]{1,0:T(8,128)S(1)}) custom-call(s32[384]{0:T(512)} %act_hbm.1, s32[16,4,384]{2,1,0:T(4,128)} %bitcast.1, bf16[512,2048]{1,0:T(8,128)(2,1)} %alpha_hbm.1, bf16[16,32,2048]{2,1,0:T(8,128)(2,1)} %trans_hbm.1, f32[4,16,2048]{2,1,0:T(8,128)} %obs_hbm.1, f32[16,2048]{1,0:T(8,128)} %rew_hbm.1), custom_call_target="tpu_custom_call" | custom-call | tf_op jit(solution)/shard_map/backup/pallas_call | solution.py:709
  49.2 0.6 %multiply_add_fusion = f32[6,2048]{1,0:T(8,128)} fusion(f32[6,2048]{1,0:T(8,128)S(1)} %get-tuple-element.7, f32[6,2048]{1,0:T(8,128)S(1)} %get-tuple-element.8), kind=kLoop, calls=%fused_computation | loop fusion | flops 24576 | bytes 147456 | tf_op jit(solution)/shard_map/add | solution.py:734

commit v13 on v12

--- a/solution.py
+++ b/solution.py
@@ -201,21 +201,6 @@
     own_ts.start()
     own_rew.start()
 
-    for cp in own_act:
-        cp.wait()
-    act_row = act_v[...].reshape(1, bel)
-    picks = jnp.zeros((obs_local, bel), jnp.int32)
-    for a in range(actions):
-        picks = jnp.where(act_row == a, idx_v[a] * halves, picks)
-    for o in range(obs_local):
-        pk_own[o] = picks[o : o + 1, :]
-        pk_v[z, o] = picks[o : o + 1, :]
-
-    own_ob.wait()
-    for n in range(nz):
-        for o in range(obs_local):
-            v = jnp.log(obs_v[o, :, n * width : (n + 1) * width])
-            obs_code[n, o] = jnp.round(v * CODE_SCALE + CODE_SHIFT).astype(jnp.int32).astype(jnp.int16)
     pl.semaphore_wait(barrier, len(peers))
 
     quarter = half_y // 2
@@ -268,8 +253,6 @@
 
     ts_cp = [trans_copy(t, mine, ts_send, ts_recv) for t in range(ng - 1)]
     t_cp = [trans_copy(t, pl.ds(0, direct), t_send, t_recv) for t in range(ng - 1)]
-    for cp in pk_cp:
-        cp.start()
     own_al.wait()
     across = lax.rem(y + ny - 2, ny)
     relay_cp = [
@@ -288,12 +271,29 @@
             pair[m].start()
     for m in range(2):
         relay_cp[m].start()
+    for cp in ts_cp:
+        cp.start()
+    for cp in t_cp:
+        cp.start()
+
+    for cp in own_act:
+        cp.wait()
+    act_row = act_v[...].reshape(1, bel)
+    picks = jnp.zeros((obs_local, bel), jnp.int32)
+    for a in range(actions):
+        picks = jnp.where(act_row == a, idx_v[a] * halves, picks)
+    for o in range(obs_local):
+        pk_own[o] = picks[o : o + 1, :]
+        pk_v[z, o] = picks[o : o + 1, :]
+    for cp in pk_cp:
+        cp.start()
+    own_ob.wait()
+    for n in range(nz):
+        for o in range(obs_local):
+            v = jnp.log(obs_v[o, :, n * width : (n + 1) * width])
+            obs_code[n, o] = jnp.round(v * CODE_SCALE + CODE_SHIFT).astype(jnp.int32).astype(jnp.int16)
     for t in far_first(nz):
         ob_cp[t].start()
-    for cp in ts_cp:
-        cp.start()
-    for cp in t_cp:
-        cp.start()
 
     def spread_alpha(block, start, rows):
         def rows16(n, carry):
@@ -495,13 +495,18 @@
         values.append(raw / divisor)
     coded, level = to_codes(values)
     for h in range(halves):
-        cols = slice(h * LANES, (h + 1) * LANES)
-        w_all[g, :own_rows, cols] = coded[h].astype(jnp.int16)
-        w_all[g, own_rows:, cols] = level.astype(jnp.int16)
+        w_all[g, h * own_rows : (h + 1) * own_rows, :] = coded[h].astype(jnp.int16)
+    w_used = halves * own_rows
+    w_all[g, w_used : w_used + 8, :] = level.astype(jnp.int16)
 
     w_cp = [
         pltpu.make_async_remote_copy(
-            w_all.at[g], w_all.at[g], w_send.at[t], w_recv.at[t], device_id=to_g(t), device_id_type=MESH
+            w_all.at[g, pl.ds(0, w_used + 2)],
+            w_all.at[g, pl.ds(0, w_used + 2)],
+            w_send.at[t],
+            w_recv.at[t],
+            device_id=to_g(t),
+            device_id_type=MESH,
         )
         for t in range(ng - 1)
     ]
@@ -511,13 +516,13 @@
     def spread_owner(j):
         rows = pl.ds(pl.multiple_of(j * own_rows, own_rows), own_rows)
         low_rows = pl.ds(pl.multiple_of(bel + j * own_rows, own_rows), own_rows)
-        w_scale[rows, :] = jnp.broadcast_to(
-            scale_of(w_all[j, own_rows : own_rows + 1, :].astype(jnp.int32).astype(jnp.float32)), (own_rows, width)
-        )[:, :qwidth]
+        scale = scale_of(w_all[j, w_used : w_used + 1, :].astype(jnp.int32).astype(jnp.float32))
+        for h in range(qwidth // LANES):
+            w_scale[rows, h * LANES : (h + 1) * LANES] = jnp.broadcast_to(scale, (own_rows, LANES))
         act = act_b[rows, :]
         pieces = []
         for h in range(halves):
-            q = w_all[j, :own_rows, h * LANES : (h + 1) * LANES].astype(jnp.int32)
+            q = w_all[j, h * own_rows : (h + 1) * own_rows, :].astype(jnp.int32)
             high = jnp.right_shift(q + 128, 8)
             low = q - jnp.left_shift(high, 8)
             pieces.append((high.astype(jnp.float32).astype(jnp.bfloat16), low.astype(jnp.float32).astype(jnp.bfloat16)))
@@ -663,7 +668,7 @@
         pltpu.VMEM((dims[2], own_rows * halves, LANES), f32),
         pltpu.VMEM((halves, actions, LANES), f32),
         pltpu.VMEM((ng - 1, halves, actions, LANES), f32),
-        pltpu.VMEM((ng, own_rows + 8, width), jnp.int16),
+        pltpu.VMEM((ng, halves * own_rows + 16, LANES), jnp.int16),
         pltpu.VMEM((actions, width, qwidth), b16),
         pltpu.VMEM((2 * bel, actions * width), b16),
         pltpu.VMEM((bel, qwidth), f32),

time: 49.9 us -> 49.5 us (level)
  no operation moved by 1% of the time
where the time goes in v13:
time: 49.5 us; the launch traced here: 49.4 us
  Pallas kernels  48.8 us (99%)
  other arithmetic  0.64 us (1%)
    pallas_call x1, Pallas kernels, body(): pl.pallas_call(functools.partial(kernel, dims), out_shape=(rows, rows), i...  48.8 us

profile of v13, /device:TPU:1, one launch (start us, length us, event | category | flops | bytes accessed | tf_op | source)
XLA Modules:
  0.0 49.4 jit_solution(15158560263747627655)
XLA Ops:
  0.0 48.8 %backup.1 = (f32[6,2048]{1,0:T(8,128)S(1)}, f32[6,2048]{1,0:T(8,128)S(1)}) custom-call(s32[384]{0:T(512)} %act_hbm.1, s32[16,4,384]{2,1,0:T(4,128)} %bitcast.1, bf16[512,2048]{1,0:T(8,128)(2,1)} %alpha_hbm.1, bf16[16,32,2048]{2,1,0:T(8,128)(2,1)} %trans_hbm.1, f32[4,16,2048]{2,1,0:T(8,128)} %obs_hbm.1, f32[16,2048]{1,0:T(8,128)} %rew_hbm.1), custom_call_target="tpu_custom_call" | custom-call | tf_op jit(solution)/shard_map/backup/pallas_call | solution.py:714
  48.8 0.6 %multiply_add_fusion = f32[6,2048]{1,0:T(8,128)} fusion(f32[6,2048]{1,0:T(8,128)S(1)} %get-tuple-element.7, f32[6,2048]{1,0:T(8,128)S(1)} %get-tuple-element.8), kind=kLoop, calls=%fused_computation | loop fusion | flops 24576 | bytes 147456 | tf_op jit(solution)/shard_map/add | solution.py:739
